TPU v7x, 32 devices: a whole 2x2x4 slice. The times are simulated.
32 devices in a mesh: dp: 2 (over x), tp: 4 (over z), sp: 4 (over y, core).
Axes of the slice: x: 2, y: 2, z: 4, core: 2. Of those that a mesh axis runs over, the one named last changes fastest.
Arguments:
- tokens: bfloat16 [128, 2560], P('dp'), parts along dimension 0
- positions: int32 [128], P('dp'), parts along dimension 0
- cache_k: bfloat16 [128, 1024, 4, 256], P('dp', 'sp', 'tp'), parts along dimension 0
- cache_v: bfloat16 [128, 1024, 4, 256], P('dp', 'sp', 'tp'), parts along dimension 0
- attn_gain: bfloat16 [2560], replicated
- w_q: bfloat16 [2560, 2048], P(None, 'tp')
- w_k: bfloat16 [2560, 1024], P(None, 'tp')
- w_v: bfloat16 [2560, 1024], P(None, 'tp')
- w_o: bfloat16 [2048, 2560], P('tp')
- mlp_gain: bfloat16 [2560], replicated
- w_gate: bfloat16 [2560, 10240], P(None, 'tp')
- w_up: bfloat16 [2560, 10240], P(None, 'tp')
- w_down: bfloat16 [10240, 2560], P('tp')
Outputs:
- output 1: bfloat16 [128, 2560], P('dp'), parts along dimension 0
- output 2: bfloat16 [128, 1024, 4, 256], P('dp', 'sp', 'tp'), parts along dimension 0
- output 3: bfloat16 [128, 1024, 4, 256], P('dp', 'sp', 'tp'), parts along dimension 0
There are 2 independent parts. A program takes and returns all parts, laid end to end along the dimension named above; an argument that names none is the same for every part.
All inputs are finite; a program needn't handle non-finite values.
Results may differ from a plain program's by a relative error of at most 0.00832149.
Values sent between devices are 32-bit elements.
A program may use at most 1 GiB of HBM per device.

v0:
```python
import math
import jax
import jax.numpy as jnp
from jax import lax
from jax.sharding import PartitionSpec as P

NORM_EPS = 1e-5
ROPE_THETA = 10000.0


def rms_norm(values, gain):
    wide = values.astype(jnp.float32)
    inv_rms = lax.rsqrt(jnp.mean(wide * wide, axis=-1, keepdims=True) + NORM_EPS)
    return (wide * inv_rms * gain.astype(jnp.float32)).astype(jnp.bfloat16)


def rope_tables(positions, head_dim):
    frequencies = ROPE_THETA ** (-2.0 * jnp.arange(head_dim // 2, dtype=jnp.float32) / head_dim)
    angles = positions.astype(jnp.float32)[:, None] * frequencies[None, :]
    return jnp.cos(angles)[:, None, :], jnp.sin(angles)[:, None, :]


def apply_rope(vectors, cos_table, sin_table):
    half = vectors.shape[-1] // 2
    first = vectors[..., :half]
    second = vectors[..., half:]
    return jnp.concatenate([first * cos_table - second * sin_table, second * cos_table + first * sin_table], axis=-1)


def solution(mesh):
    sp_size = mesh.shape["sp"]
    cache_spec = P("dp", "sp", "tp", None)
    row_spec = P("dp", None)
    col_spec = P(None, "tp")
    in_specs = (row_spec, P("dp"), cache_spec, cache_spec, P(None), col_spec, col_spec, col_spec, P("tp", None), P(None), col_spec, col_spec, P("tp", None))
    out_specs = (row_spec, cache_spec, cache_spec)

    def local_step(tokens, positions, cache_k, cache_v, attn_gain, w_q, w_k, w_v, w_o, mlp_gain, w_gate, w_up, w_down):
        rows = tokens.shape[0]
        local_slots = cache_k.shape[1]
        kv_local = cache_k.shape[2]
        head_dim = cache_k.shape[3]
        heads_local = w_q.shape[1] // head_dim
        group = heads_local // kv_local
        slots = local_slots * sp_size
        slot_ids = lax.axis_index("sp") * local_slots + jnp.arange(local_slots)

        normed = rms_norm(tokens, attn_gain)
        cos_table, sin_table = rope_tables(positions, head_dim)
        q_lin = jnp.dot(normed, w_q, preferred_element_type=jnp.float32).reshape(rows, heads_local, head_dim)
        k_lin = jnp.dot(normed, w_k, preferred_element_type=jnp.float32).reshape(rows, kv_local, head_dim)
        v_new = jnp.dot(normed, w_v, preferred_element_type=jnp.float32).astype(jnp.bfloat16).reshape(rows, kv_local, head_dim)
        q_rot = apply_rope(q_lin, cos_table, sin_table).astype(jnp.bfloat16).reshape(rows, kv_local, group, head_dim)
        k_rot = apply_rope(k_lin, cos_table, sin_table).astype(jnp.bfloat16)

        hit_mask = (slot_ids[None, :] == (positions % slots)[:, None])[:, :, None, None]
        new_k = jnp.where(hit_mask, k_rot[:, None], cache_k)
        new_v = jnp.where(hit_mask, v_new[:, None], cache_v)

        scores = jnp.einsum("bkgd,bskd->bkgs", q_rot, new_k, preferred_element_type=jnp.float32) * (1.0 / math.sqrt(head_dim))
        valid = ((positions[:, None] >= slots - 1) | (slot_ids[None, :] <= positions[:, None]))[:, None, None, :]
        local_max = jnp.max(jnp.where(valid, scores, -jnp.inf), axis=-1)
        exp_scores = jnp.exp(jnp.where(valid, scores - local_max[..., None], -jnp.inf))
        local_sum = jnp.sum(exp_scores, axis=-1)
        local_out = jnp.einsum("bkgs,bskd->bkgd", exp_scores.astype(jnp.bfloat16), new_v, preferred_element_type=jnp.float32)

        global_max = lax.pmax(local_max, "sp")
        factor = jnp.exp(local_max - global_max)
        packed = jnp.concatenate([local_out * factor[..., None], (local_sum * factor)[..., None]], axis=-1)
        total = lax.psum(packed, "sp")
        attended = (total[..., :head_dim] / total[..., head_dim:]).astype(jnp.bfloat16).reshape(rows, heads_local * head_dim)

        attn_proj = lax.psum(jnp.dot(attended, w_o, preferred_element_type=jnp.float32), "tp")
        hidden = (tokens.astype(jnp.float32) + attn_proj).astype(jnp.bfloat16)
        normed_mlp = rms_norm(hidden, mlp_gain)
        gate_proj = jnp.dot(normed_mlp, w_gate, preferred_element_type=jnp.float32)
        up_proj = jnp.dot(normed_mlp, w_up, preferred_element_type=jnp.float32)
        activated = (jax.nn.silu(gate_proj) * up_proj).astype(jnp.bfloat16)
        mlp_down = lax.psum(jnp.dot(activated, w_down, preferred_element_type=jnp.float32), "tp")
        layer_out = (hidden.astype(jnp.float32) + mlp_down).astype(jnp.bfloat16)
        return layer_out, new_k, new_v

    return jax.shard_map(local_step, mesh=mesh, in_specs=in_specs, out_specs=out_specs, check_vma=False)
```

profile of v0, /device:TPU:0, one launch (start us, length us, event | category | flops | bytes accessed | tf_op | source)
XLA Modules:
  0.0 197.7 jit_solution(8753769993427342983)
XLA Ops:
  7.2 0.0 copy-start
  7.2 0.0 all-reduce.4.cloned.1.call-start
  7.2 0.8 broadcast_compare_fusion.1
  8.1 0.7 fusion.55
  8.8 1.1 fusion.14
  10.0 0.7 convert_element_type.53
  10.7 1.8 convolution_convert_fusion
  12.5 1.8 convolution_bitcast_fusion
  14.3 0.2 multiply_cosine_fusion.1
  14.5 0.2 fusion.42
  14.7 2.5 %fusion.52 = f32[64,512]{1,0:T(8,128)S(1)} fusion(bf16[2560,512]{1,0:T(8,128)(2,1)} %param.18, bf16[64,2560]{1,0:T(8,128)(2,1)} %param.13, f32[2560]{0:T(1024)S(1)} %convert_element_type.53, f32[64]{0:T(128)S(1)} %add_rsqrt_fusion.1), kind=kOutput, calls=%fused_computation.75 | convolution fusion | flops 168427520 | bytes 3090688 | tf_op jit(solution)/shard_map/dot_general | solution.py:50
  17.2 0.1 reshape.268
  17.3 0.8 compare_or_fusion
  18.1 0.1 subtract_convert_fusion
  18.1 9.8 %broadcast_select_fusion = (bf16[64,256,1,256]{3,1,2,0:T(8,128)(2,1)}, bf16[64,256,1,256]{3,1,2,0:T(8,128)(2,1)S(1)}) fusion(bf16[64,256,1,256]{3,1,2,0:T(8,128)(2,1)} %param.16, pred[64,256]{1,0:T(8,128)(4,1)S(1)} %get-tuple-element.14, bf16[64,256]{1,0:T(8,128)(2,1)S(1)} %convolution_convert_fusion, bf16[64,256,1,256]{3,1,2,0:T(8,128)(2,1)} %param.15, ...), kind=kLoop, calls=%fused_computation.4 | loop fusion | flops 8388608 | bytes 33636352 | tf_op jit(solution)/shard_map/jit(_where)/select_n | solution.py:58
  27.9 0.0 copy-start.1
  27.9 3.4 %copy-done.1 = bf16[64,256,1,256]{3,1,2,0:T(8,128)(2,1)} copy-done((bf16[64,256,1,256]{3,1,2,0:T(8,128)(2,1)}, bf16[64,256,1,256]{3,1,2,0:T(8,128)(2,1)S(1)}, u32[]{:S(2)}) %copy-start.1) | copy-done | bytes 8388632
  31.3 2.3 %select_reduce_fusion = (f32[64,2]{1,0:T(8,128)S(1)}, f32[64,2,256]{2,1,0:T(2,128)S(1)}) fusion(pred[64,256]{1,0:T(8,128)(4,1)S(1)} %get-tuple-element.13, bf16[64,256,1,256]{3,1,2,0:T(8,128)(2,1)S(1)} %get-tuple-element.10, bf16[64,2,128]{2,1,0:T(2,128)(2,1)S(1)} %get-tuple-element.6, bf16[64,2,128]{2,1,0:T(2,128)(2,1)S(1)} %get-tuple-element.5), kind=kOutput, calls=%fused_computation.32 | convolution fusion | flops 17006464 | bytes 8602112 | tf_op jit(solution)/shard_map/bkgd,bskd->bkgs/dot_general | solution.py:60
  33.6 0.0 copy-start.3
  33.6 0.0 copy-start.2
  33.6 0.1 copy.21
  33.7 8.5 %pmax.7 = f32[64,1,2]{0,2,1:T(2,128)S(1)} all-reduce(f32[64,1,2]{0,2,1:T(2,128)S(1)} %bitcast.48), channel_id=1, replica_groups=mesh['dp'=2,'tp'=4,'sp'=4] {'sp'}, use_global_device_ids=true, to_apply=%region_2.3 | all-reduce | flops 128 | bytes 1024 | tf_op jit(solution)/shard_map/pmax | solution.py:67
  42.3 0.3 fusion.43
  42.6 0.1 copy.23
  42.6 0.1 copy.22
  42.7 0.1 copy.24
  42.9 4.6 %fusion.11 = f32[64,1,2,256]{3,2,0,1:T(2,128)S(1)} fusion(bf16[64,256,1,256]{3,1,2,0:T(8,128)(2,1)} %get-tuple-element.9, f32[64,2]{1,0:T(8,128)S(1)} %copy.22, f32[64,2,256]{2,1,0:T(2,128)S(1)} %get-tuple-element.20, pred[64,256]{1,0:T(8,128)(4,1)S(1)} %get-tuple-element.13, f32[64,2]{1,0:T(8,128)S(1)} %get-tuple-element.19), kind=kOutput, calls=%fused_computation.12 | convolution fusion | flops 16908288 | bytes 8668160 | tf_op jit(solution)/shard_map/bkgs,bskd->bkgd/dot_general | solution.py:65
  47.5 0.8 pad_maximum_fusion
  48.3 0.0 all-reduce.4.cloned.1.call-update
  48.3 0.0 all-reduce.6.cloned.1.call-start
  48.4 32.4 %all-reduce.4.cloned.1.call-done = f32[64,1,2,257]{3,2,0,1:T(2,128)} async-done(((f32[64,1,2,257]{3,2,0,1:T(2,128)}), f32[64,1,2,257]{3,2,0,1:T(2,128)}) %all-reduce.4.cloned.1.call-update) | async-done | bytes 131600 | tf_op jit(solution)/shard_map/psum | solution.py:70
  80.8 0.8 slice.29
  81.6 0.1 copy.25
  81.7 0.1 copy.26
  81.8 1.0 fusion.24
  82.9 0.0 copy-done
  82.9 1.4 fusion.56
  84.3 0.0 all-reduce.6.cloned.1.call-update
  84.3 0.0 all-reduce.8.cloned.1.call-start
  84.4 0.0 copy-done.3
  84.4 40.8 %all-reduce.6.cloned.1.call-done = f32[64,2560]{1,0:T(8,128)} async-done(((f32[64,2560]{1,0:T(8,128)}), f32[64,2560]{1,0:T(8,128)}) %all-reduce.6.cloned.1.call-update) | async-done | bytes 655376 | tf_op jit(solution)/shard_map/psum | solution.py:73
  125.2 0.0 copy-done.2
  125.2 1.3 fusion.18
  126.5 8.0 %fusion.27 = f32[64,2560]{1,0:T(8,128)} fusion(bf16[2560,2560]{1,0:T(8,128)(2,1)} %param.23, bf16[64,2560]{1,0:T(8,128)(2,1)S(1)} %get-tuple-element.4, f32[2560]{0:T(1024)S(1)} %convert_element_type.61, f32[64]{0:T(128)S(1)} %add_rsqrt_fusion), kind=kOutput, calls=%fused_computation.34 | convolution fusion | flops 839516160 | bytes 14100736 | tf_op jit(solution)/shard_map/dot_general | solution.py:76
  134.6 14.3 %fusion.22 = f32[64,2560]{1,0:T(8,128)} fusion(bf16[2560,2560]{1,0:T(8,128)(2,1)} %param.25, bf16[2560,2560]{1,0:T(8,128)(2,1)} %param.24, f32[64,2560]{1,0:T(8,128)} %fusion.27, bf16[64,2560]{1,0:T(8,128)(2,1)S(1)} %get-tuple-element.4, f32[2560]{0:T(1024)S(1)} %convert_element_type.61, f32[64]{0:T(128)S(1)} %add_rsqrt_fusion), kind=kOutput, calls=%fused_computation.27 | convolution fusion | flops 1679360000 | bytes 27863296 | tf_op jit(solution)/shard_map/dot_general | solution.py:79
  148.9 0.0 all-reduce.8.cloned.1.call-update
  148.9 40.4 %all-reduce.8.cloned.1.call-done = f32[64,2560]{1,0:T(8,128)} async-done(((f32[64,2560]{1,0:T(8,128)}), f32[64,2560]{1,0:T(8,128)}) %all-reduce.8.cloned.1.call-update) | async-done | bytes 655376 | tf_op jit(solution)/shard_map/psum | solution.py:79
  189.3 1.9 fusion.21
  (8 shorter events, 0.1 us)
Async XLA Ops:
  7.2 75.7 %copy-start = (bf16[512,2560]{1,0:T(8,128)(2,1)S(1)}, bf16[512,2560]{1,0:T(8,128)(2,1)}, u32[]{:S(2)}) copy-start(bf16[512,2560]{1,0:T(8,128)(2,1)} %param.21) | copy-start | bytes 7864324
  7.2 73.6 %all-reduce.4.cloned.1.call-start = ((), (), s32[]{:S(2)}) async-start(), calls=%async_computation | async-start | bytes 393216 | tf_op jit(solution)/shard_map/psum | solution.py:70
  27.9 3.4 %copy-start.1 = (bf16[64,256,1,256]{3,1,2,0:T(8,128)(2,1)}, bf16[64,256,1,256]{3,1,2,0:T(8,128)(2,1)S(1)}, u32[]{:S(2)}) copy-start(bf16[64,256,1,256]{3,1,2,0:T(8,128)(2,1)S(1)} %get-tuple-element.10) | copy-start | bytes 25165828
  33.6 50.7 %copy-start.3 = (bf16[2560]{0:T(1024)(128)(2,1)S(1)}, bf16[2560]{0:T(1024)(128)(2,1)}, u32[]{:S(2)}) copy-start(bf16[2560]{0:T(1024)(128)(2,1)} %param.22) | copy-start | bytes 15364
  33.6 91.6 %copy-start.2 = (bf16[64,2560]{1,0:T(8,128)(2,1)S(1)}, bf16[64,2560]{1,0:T(8,128)(2,1)}, u32[]{:S(2)}) copy-start(bf16[64,2560]{1,0:T(8,128)(2,1)} %param.13) | copy-start | bytes 983044
  48.3 76.9 %all-reduce.6.cloned.1.call-start = ((), (), s32[]{:S(2)}) async-start(), calls=%async_computation.1 | async-start | bytes 1310720 | tf_op jit(solution)/shard_map/psum | solution.py:73
  84.3 105.0 %all-reduce.8.cloned.1.call-start = ((), (), s32[]{:S(2)}) async-start(), calls=%async_computation.2 | async-start | bytes 1310720 | tf_op jit(solution)/shard_map/psum | solution.py:79
Sparse Core Ops, SparseCore 0:
  48.5 32.2 all-reduce.3
  84.4 40.7 all-reduce.5
  149.0 40.2 all-reduce.7
where the time goes:
time: 198 us
  waiting for transfers between devices  114 us (58%)
  matrix products  36.8 us (19%)
  other arithmetic  19.7 us (10%)
  between operations  13.9 us (7%)
  blocking collectives  8.55 us (4%)
  local copies, waits for them, and re-layouts  4.91 us (2%)
    psum x1, waiting for transfers between devices, local_step(): lax.psum(jnp.dot(attended, w_o, preferred_element_type=jnp.float32), 'tp')  40.8 us
    psum x1, waiting for transfers between devices, local_step(): lax.psum(jnp.dot(activated, w_down, preferred_element_type=jnp.float32),...  40.4 us
    psum x1, waiting for transfers between devices, local_step(): total = lax.psum(packed, 'sp')  32.4 us
    dot_general x1, matrix products, local_step(): jnp.dot(activated, w_down, preferred_element_type=jnp.float32)  14.3 us
    select_n x1, other arithmetic, local_step(): new_v = jnp.where(hit_mask, v_new[:, None], cache_v)  9.76 us
    pmax x1, blocking collectives, local_step(): global_max = lax.pmax(local_max, 'sp')  8.55 us
    dot_general x1, matrix products, local_step(): gate_proj = jnp.dot(normed_mlp, w_gate, preferred_element_type=jnp.float32)  8.04 us
    dot_general x1, matrix products, local_step(): jnp.einsum('bkgs,bskd->bkgd', exp_scores.astype(jnp.bfloat16), new_v, pre...  4.64 us
  transfers between devices with their start and end apart: 3, of which 3 were waited for; matrix products, arithmetic and copies ran while one was open for 0% of the time, Pallas kernels for 0%

commit v1 on v0

v1 whole, which is shorter than its diff:
```python
import functools
import math

import jax
import jax.numpy as jnp
import numpy as np
from jax import lax
from jax.experimental import pallas as pl
from jax.experimental.pallas import tpu as pltpu
from jax.sharding import PartitionSpec as P

NORM_EPS = 1e-5
ROPE_THETA = 10000.0
F32 = jnp.float32
BF16 = jnp.bfloat16
CHUNK = 16


def rms_norm(values, gain):
    wide = values.astype(F32)
    inv_rms = lax.rsqrt(jnp.mean(wide * wide, axis=-1, keepdims=True) + NORM_EPS)
    return (wide * inv_rms * gain.astype(F32)).astype(BF16)


def attn_kernel(sp_size, pos_ref, freq_ref, tok_hbm, gain_hbm, wq_hbm, wk_hbm, wv_hbm, ck_hbm, cv_hbm,
                nk_hbm, nv_hbm, part_ref, nk_ref, nv_ref, tok, gain, wq, wk, wv, qs, knew, vnew, posm,
                sem_w, sem_k, sem_v, sem_ko, sem_vo):
    rows = tok.shape[0]
    local_slots = nk_ref.shape[1]
    dim = nk_ref.shape[2]
    half = dim // 2
    slots = local_slots * sp_size
    chunks = rows // CHUNK
    base = lax.axis_index("sp") * local_slots

    loads = [pltpu.make_async_copy(src, dst, sem_w.at[i]) for i, (src, dst) in enumerate(
        ((tok_hbm, tok), (gain_hbm, gain), (wk_hbm, wk), (wv_hbm, wv), (wq_hbm, wq)))]
    for copy in loads:
        copy.start()
    k_loads, v_loads, k_stores, v_stores = [], [], [], []
    for c in range(chunks):
        span = pl.ds(c * CHUNK, CHUNK)
        k_loads.append(pltpu.make_async_copy(ck_hbm.at[span], nk_ref.at[span], sem_k.at[c]))
        v_loads.append(pltpu.make_async_copy(cv_hbm.at[span], nv_ref.at[span], sem_v.at[c]))
        k_stores.append(pltpu.make_async_copy(nk_ref.at[span], nk_hbm.at[span], sem_ko.at[c]))
        v_stores.append(pltpu.make_async_copy(nv_ref.at[span], nv_hbm.at[span], sem_vo.at[c]))
        k_loads[c].start()
        v_loads[c].start()

    sub = lax.broadcasted_iota(jnp.int32, (8, 128), 0)
    for g in range(rows // 8):
        acc = jnp.zeros((8, 128), jnp.int32)
        for r in range(8):
            acc = jnp.where(sub == r, pos_ref[8 * g + r], acc)
        posm[pl.ds(8 * g, 8), :] = acc
    angles = posm[...].astype(F32) * freq_ref[...]
    cos = jnp.cos(angles)
    sin = jnp.sin(angles)

    loads[0].wait()
    loads[1].wait()
    wide = tok[...].astype(F32)
    inv_rms = lax.rsqrt(jnp.mean(wide * wide, axis=-1, keepdims=True) + NORM_EPS)
    normed = (wide * inv_rms * gain[...].astype(F32).reshape(1, -1)).astype(BF16)

    def rope(lin):
        a, b = lin[:, :half], lin[:, half:]
        return jnp.concatenate([a * cos - b * sin, b * cos + a * sin], axis=-1)

    loads[2].wait()
    knew[...] = rope(jnp.dot(normed, wk[...], preferred_element_type=F32)).astype(BF16).astype(F32)
    loads[3].wait()
    vnew[...] = jnp.dot(normed, wv[...], preferred_element_type=F32).astype(BF16).astype(F32)
    loads[4].wait()
    heads = wq.shape[1] // dim
    q_lin = jnp.dot(normed, wq[...], preferred_element_type=F32)
    q_rot = [rope(q_lin[:, h * dim:(h + 1) * dim]) for h in range(heads)]
    for g in range(rows // 8):
        qs[g] = jnp.concatenate([q_rot[h][8 * g:8 * g + 8] for h in range(heads)], axis=0).astype(BF16)

    sub16 = lax.broadcasted_iota(jnp.int32, (16, dim), 0)
    lane = lax.broadcasted_iota(jnp.int32, (16, local_slots), 1) + base
    lane128 = lax.broadcasted_iota(jnp.int32, (16, 128), 1)

    def patch(ref, new_ref, b, offset):
        inside = jnp.clip(offset, 0, local_slots - 1)
        start = pl.multiple_of((inside // 16) * 16, 16)
        old = ref[b, pl.ds(start, 16), :].astype(F32)
        ref[b, pl.ds(start, 16), :] = jnp.where(sub16 == offset - start, new_ref[pl.ds(b, 1), :], old).astype(BF16)

    for c in range(chunks):
        offsets = [jnp.bitwise_and(pos_ref[c * CHUNK + j], slots - 1) - base for j in range(CHUNK)]
        k_loads[c].wait()
        for j in range(CHUNK):
            patch(nk_ref, knew, c * CHUNK + j, offsets[j])
        k_stores[c].start()
        probs = []
        for g in range(c * CHUNK // 8, (c + 1) * CHUNK // 8):
            query = qs[g]
            scores = jnp.zeros((16, local_slots), F32)
            for j in range(8):
                one = lax.dot_general(query, nk_ref[8 * g + j], (((1,), (1,)), ((), ())), preferred_element_type=F32)
                scores = jnp.where(jnp.bitwise_and(sub16, 7) == j, one, scores)
            scores = scores * (1.0 / math.sqrt(dim))
            pos8 = posm[pl.ds(8 * g, 8), :]
            pos16 = jnp.concatenate([pos8, pos8], axis=0)
            limit = jnp.where(pos16 >= slots - 1, slots, pos16)
            valid = lane <= jnp.concatenate([limit] * (local_slots // 128), axis=1)
            top = jnp.max(jnp.where(valid, scores, -jnp.inf), axis=-1, keepdims=True)
            safe = jnp.where(top == -jnp.inf, 0.0, top)
            weights = jnp.exp(jnp.where(valid, scores - safe, -jnp.inf))
            total = jnp.sum(weights, axis=-1, keepdims=True)
            probs.append((g, weights.astype(BF16), top, total))
        v_loads[c].wait()
        for j in range(CHUNK):
            patch(nv_ref, vnew, c * CHUNK + j, offsets[j])
        v_stores[c].start()
        for g, weights, top, total in probs:
            out = jnp.zeros((16, dim), F32)
            for j in range(8):
                one = jnp.dot(weights, nv_ref[8 * g + j], preferred_element_type=F32)
                out = jnp.where(jnp.bitwise_and(sub16, 7) == j, one, out)
            stats = jnp.where(lane128 < 64, top, total)
            dest, upper = g // 2, g % 2
            for h in range(heads):
                span = pl.ds(16 * h + 8 * upper, 8)
                part_ref[dest, span, 0:dim] = out[8 * h:8 * h + 8]
                part_ref[dest, span, dim:dim + 128] = stats[8 * h:8 * h + 8]
    for copy in k_stores + v_stores:
        copy.wait()


def attend(tokens, positions, cache_k, cache_v, gain, w_q, w_k, w_v, sp_size):
    rows, width = tokens.shape
    _, local_slots, _, dim = cache_k.shape
    heads = w_q.shape[1] // dim
    freq = (ROPE_THETA ** (-2.0 * np.arange(dim // 2, dtype=np.float64) / dim)).astype(np.float32)
    ck = cache_k.reshape(rows, local_slots, dim)
    cv = cache_v.reshape(rows, local_slots, dim)
    any_spec = pl.BlockSpec(memory_space=pltpu.HBM)
    vmem_spec = pl.BlockSpec(memory_space=pltpu.VMEM)
    chunks = rows // CHUNK
    nk, nv, part = pl.pallas_call(
        functools.partial(attn_kernel, sp_size),
        name="attend",
        out_shape=(
            jax.ShapeDtypeStruct((rows, local_slots, dim), BF16),
            jax.ShapeDtypeStruct((rows, local_slots, dim), BF16),
            jax.ShapeDtypeStruct((sp_size, heads * rows // sp_size, dim + 128), F32),
        ),
        in_specs=[pl.BlockSpec(memory_space=pltpu.SMEM), vmem_spec] + [any_spec] * 7,
        out_specs=[any_spec, any_spec, vmem_spec],
        scratch_shapes=[
            pltpu.VMEM((rows, local_slots, dim), BF16),
            pltpu.VMEM((rows, local_slots, dim), BF16),
            pltpu.VMEM((rows, width), BF16),
            pltpu.VMEM((width,), BF16),
            pltpu.VMEM(w_q.shape, BF16),
            pltpu.VMEM(w_k.shape, BF16),
            pltpu.VMEM(w_v.shape, BF16),
            pltpu.VMEM((rows // 8, 8 * heads, dim), BF16),
            pltpu.VMEM((rows, dim), F32),
            pltpu.VMEM((rows, dim), F32),
            pltpu.VMEM((rows, 128), jnp.int32),
            pltpu.SemaphoreType.DMA((5,)),
            pltpu.SemaphoreType.DMA((chunks,)),
            pltpu.SemaphoreType.DMA((chunks,)),
            pltpu.SemaphoreType.DMA((chunks,)),
            pltpu.SemaphoreType.DMA((chunks,)),
        ],
        compiler_params=pltpu.CompilerParams(vmem_limit_bytes=VMEM_A),
        cost_estimate=pl.CostEstimate(flops=2 * rows * width * 1024, bytes_accessed=22 << 20, transcendentals=0),
    )(positions, jnp.asarray(freq).reshape(1, -1), tokens, gain, w_q, w_k, w_v, ck, cv)
    return nk.reshape(cache_k.shape), nv.reshape(cache_v.shape), part


VMEM_A = 67043328 - (448 << 10)


def solution(mesh):
    sp_size = mesh.shape["sp"]
    cache_spec = P("dp", "sp", "tp", None)
    row_spec = P("dp", None)
    col_spec = P(None, "tp")
    in_specs = (row_spec, P("dp"), cache_spec, cache_spec, P(None), col_spec, col_spec, col_spec, P("tp", None), P(None), col_spec, col_spec, P("tp", None))
    out_specs = (row_spec, cache_spec, cache_spec)

    def local_step(tokens, positions, cache_k, cache_v, attn_gain, w_q, w_k, w_v, w_o, mlp_gain, w_gate, w_up, w_down):
        rows = tokens.shape[0]
        dim = cache_k.shape[3]
        new_k, new_v, part = attend(tokens, positions, cache_k, cache_v, attn_gain, w_q, w_k, w_v, sp_size)
        o = part[:, :, :dim]; m = part[:, :, dim:dim + 1]; l = part[:, :, dim + 64:dim + 65]
        gm = lax.pmax(m, "sp")
        f = jnp.exp(m - gm)
        tot = lax.psum(jnp.concatenate([o * f, l * f], axis=-1), "sp")
        att = (tot[..., :dim] / tot[..., dim:]).astype(BF16)
        att = att.reshape(4, 2, 16, dim).transpose(0, 2, 1, 3).reshape(rows, 2 * dim)
        attn_proj = lax.psum(jnp.dot(att, w_o, preferred_element_type=F32), "tp")
        hidden = (tokens.astype(F32) + attn_proj).astype(BF16)
        normed_mlp = rms_norm(hidden, mlp_gain)
        gate_proj = jnp.dot(normed_mlp, w_gate, preferred_element_type=F32)
        up_proj = jnp.dot(normed_mlp, w_up, preferred_element_type=F32)
        activated = (jax.nn.silu(gate_proj) * up_proj).astype(BF16)
        mlp_down = lax.psum(jnp.dot(activated, w_down, preferred_element_type=F32), "tp")
        layer_out = (hidden.astype(F32) + mlp_down).astype(BF16)
        return layer_out, new_k, new_v

    return jax.shard_map(local_step, mesh=mesh, in_specs=in_specs, out_specs=out_specs, check_vma=False)
```

time: 198 us -> 190 us (0.960)
  Pallas kernels: 0 us -> 14.9 us
  other arithmetic: 19.7 us -> 6.87 us
  matrix products: 36.8 us -> 24.4 us
  blocking collectives: 8.55 us -> 13.5 us
  local copies, waits for them, and re-layouts: 4.91 us -> 1.85 us
    pallas_call x0 -> x1, Pallas kernels: none -> 14.9 us  [attend(): pl.pallas_call(functools.partial(attn_kernel, sp_size), name='attend', ou...]
    dot_general x8 -> x3, matrix products: 36.8 us -> 24.4 us  [the longest x1 14.1 us: local_step(): jnp.dot(activated, w_down, preferred_element_type=F32)]
    select_n x1 -> x0, other arithmetic: 9.76 us -> none  [local_step(): new_v = jnp.where(hit_mask, v_new[:, None], cache_v)]
    pmax x1, blocking collectives: 8.55 us -> 13.5 us  [local_step(): gm = lax.pmax(m, 'sp')]
    unnamed x9 -> x5, local copies, waits for them, and re-layouts: 3.42 us -> 0.02 us
    convert_element_type x5 -> x3, other arithmetic: 4.35 us -> 2.87 us  [the longest x1 1.87 us: local_step(): layer_out = (hidden.astype(F32) + mlp_down).astype(BF16)]
where the time goes in v1:
time: 190 us; the launch traced here: 189 us
  waiting for transfers between devices  114 us (60%)
  matrix products  24.4 us (13%)
  Pallas kernels  14.9 us (8%)
  between operations  13.9 us (7%)
  blocking collectives  13.5 us (7%)
  other arithmetic  6.87 us (4%)
    psum x1, waiting for transfers between devices, local_step(): attn_proj = lax.psum(jnp.dot(att, w_o, preferred_element_type=F32), 'tp')  40.8 us
    psum x1, waiting for transfers between devices, local_step(): lax.psum(jnp.dot(activated, w_down, preferred_element_type=F32), 'tp')  40.4 us
    psum x1, waiting for transfers between devices, local_step(): tot = lax.psum(jnp.concatenate([o * f, l * f], axis=-1), 'sp')  32.3 us
    pallas_call x1, Pallas kernels, attend(): pl.pallas_call(functools.partial(attn_kernel, sp_size), name='attend', ou...  14.9 us
    dot_general x1, matrix products, local_step(): jnp.dot(activated, w_down, preferred_element_type=F32)  14.1 us
    pmax x1, blocking collectives, local_step(): gm = lax.pmax(m, 'sp')  13.5 us
    dot_general x1, matrix products, local_step(): gate_proj = jnp.dot(normed_mlp, w_gate, preferred_element_type=F32)  7.18 us
  transfers between devices with their start and end apart: 3, of which 3 were waited for; matrix products, arithmetic and copies ran while one was open for 0% of the time, Pallas kernels for 0%

profile of v1, /device:TPU:0, one launch (start us, length us, event | category | flops | bytes accessed | tf_op | source)
XLA Modules:
  0.0 189.2 jit_solution(10470992353070727575)
XLA Ops:
  7.2 0.0 all-reduce.4.cloned.1.call-start
  7.2 0.0 copy-start.1
  7.2 0.0 copy-start
  7.2 14.9 %attend.1 = (bf16[64,256,256]{2,1,0:T(8,128)(2,1)}, bf16[64,256,256]{2,1,0:T(8,128)(2,1)}, f32[4,32,384]{2,1,0:T(8,128)}) custom-call(s32[64]{0:T(128)} %pos_ref.1, f32[1,128]{1,0:T(1,128)} %constant.15.freq_ref, bf16[64,2560]{1,0:T(8,128)(2,1)} %tok_hbm.1, bf16[2560]{0:T(1024)(128)(2,1)} %gain_hbm.1, bf16[2560,512]{1,0:T(8,128)(2,1)} %wq_hbm.1, ...), custom_call_target="tpu_custom_call" | custom-call | flops 335544320 | bytes 23068672 | tf_op jit(solution)/shard_map/attend/pallas_call | solution.py:143
  22.2 0.8 slice.16
  23.0 13.5 %pmax.7 = f32[4,32,1]{2,1,0:T(8,128)S(1)} all-reduce(f32[4,32,1]{2,1,0:T(8,128)S(1)} %slice.16), channel_id=1, replica_groups=mesh['dp'=2,'tp'=4,'sp'=4] {'sp'}, use_global_device_ids=true, to_apply=%region_0.0 | all-reduce | flops 128 | bytes 1024 | tf_op jit(solution)/shard_map/pmax | solution.py:193
  36.5 1.0 fusion.12
  37.6 1.0 slice_multiply_fusion
  38.6 0.7 pad_maximum_fusion
  39.3 0.0 all-reduce.4.cloned.1.call-update
  39.3 0.0 all-reduce.6.cloned.1.call-start
  39.3 32.3 %all-reduce.4.cloned.1.call-done = f32[4,32,257]{2,1,0:T(8,128)} async-done(((f32[4,32,257]{2,1,0:T(8,128)}), f32[4,32,257]{2,1,0:T(8,128)}) %all-reduce.4.cloned.1.call-update) | async-done | bytes 131600 | tf_op jit(solution)/shard_map/psum | solution.py:195
  71.7 0.9 slice_reduce_fusion
  72.6 1.0 fusion.7
  73.6 0.1 copy.19
  73.7 3.2 %fusion.14 = f32[64,2560]{1,0:T(8,128)} fusion(bf16[64,512]{1,0:T(8,128)(2,1)S(1)} %bitcast.21, bf16[512,2560]{1,0:T(8,128)(2,1)} %param.22), kind=kOutput, calls=%fused_computation.23 | convolution fusion | flops 167772160 | bytes 3342336 | tf_op jit(solution)/shard_map/dot_general | solution.py:198
  76.9 0.0 all-reduce.6.cloned.1.call-update
  76.9 0.0 all-reduce.8.cloned.1.call-start
  76.9 0.0 copy-done.1
  76.9 40.8 %all-reduce.6.cloned.1.call-done = f32[64,2560]{1,0:T(8,128)} async-done(((f32[64,2560]{1,0:T(8,128)}), f32[64,2560]{1,0:T(8,128)}) %all-reduce.6.cloned.1.call-update) | async-done | bytes 655376 | tf_op jit(solution)/shard_map/psum | solution.py:198
  117.8 0.0 copy-done
  117.8 1.3 fusion.1
  119.1 7.2 %fusion.10 = f32[64,2560]{1,0:T(8,128)S(1)} fusion(bf16[2560,2560]{1,0:T(8,128)(2,1)} %param.24, bf16[64,2560]{1,0:T(8,128)(2,1)S(1)} %get-tuple-element.16, f32[2560]{0:T(1024)S(1)} %convert_element_type.29, f32[64]{0:T(128)S(1)} %add_rsqrt_fusion), kind=kOutput, calls=%fused_computation.16 | convolution fusion | flops 839516160 | bytes 14100736 | tf_op jit(solution)/shard_map/dot_general | solution.py:201
  126.3 14.1 %fusion.5 = f32[64,2560]{1,0:T(8,128)} fusion(bf16[2560,2560]{1,0:T(8,128)(2,1)} %param.26, bf16[2560,2560]{1,0:T(8,128)(2,1)} %param.25, f32[64,2560]{1,0:T(8,128)S(1)} %fusion.10, bf16[64,2560]{1,0:T(8,128)(2,1)S(1)} %get-tuple-element.16, f32[2560]{0:T(1024)S(1)} %convert_element_type.29, f32[64]{0:T(128)S(1)} %add_rsqrt_fusion), kind=kOutput, calls=%fused_computation.10 | convolution fusion | flops 1679360000 | bytes 27863296 | tf_op jit(solution)/shard_map/dot_general | solution.py:204
  140.4 0.0 all-reduce.8.cloned.1.call-update
  140.4 40.4 %all-reduce.8.cloned.1.call-done = f32[64,2560]{1,0:T(8,128)} async-done(((f32[64,2560]{1,0:T(8,128)}), f32[64,2560]{1,0:T(8,128)}) %all-reduce.8.cloned.1.call-update) | async-done | bytes 655376 | tf_op jit(solution)/shard_map/psum | solution.py:204
  180.8 1.9 fusion.4
  (3 shorter events, 0.0 us)
Async XLA Ops:
  7.2 64.5 %all-reduce.4.cloned.1.call-start = ((), (), s32[]{:S(2)}) async-start(), calls=%async_computation | async-start | bytes 393216 | tf_op jit(solution)/shard_map/psum | solution.py:195
  7.2 69.7 %copy-start.1 = (bf16[2560]{0:T(1024)(128)(2,1)S(1)}, bf16[2560]{0:T(1024)(128)(2,1)}, u32[]{:S(2)}) copy-start(bf16[2560]{0:T(1024)(128)(2,1)} %param.23) | copy-start | bytes 15364
  7.2 110.6 %copy-start = (bf16[64,2560]{1,0:T(8,128)(2,1)S(1)}, bf16[64,2560]{1,0:T(8,128)(2,1)}, u32[]{:S(2)}) copy-start(bf16[64,2560]{1,0:T(8,128)(2,1)} %tok_hbm.1) | copy-start | bytes 983044
  39.3 78.5 %all-reduce.6.cloned.1.call-start = ((), (), s32[]{:S(2)}) async-start(), calls=%async_computation.1 | async-start | bytes 1310720 | tf_op jit(solution)/shard_map/psum | solution.py:198
  76.9 103.9 %all-reduce.8.cloned.1.call-start = ((), (), s32[]{:S(2)}) async-start(), calls=%async_computation.2 | async-start | bytes 1310720 | tf_op jit(solution)/shard_map/psum | solution.py:204
Sparse Core Ops, SparseCore 0:
  39.4 32.2 all-reduce.3
  77.0 40.7 all-reduce.5
  140.5 40.2 all-reduce.7

commit v2 on v1

--- a/solution.py
+++ b/solution.py
@@ -14,12 +14,6 @@
 F32 = jnp.float32
 BF16 = jnp.bfloat16
 CHUNK = 16
-
-
-def rms_norm(values, gain):
-    wide = values.astype(F32)
-    inv_rms = lax.rsqrt(jnp.mean(wide * wide, axis=-1, keepdims=True) + NORM_EPS)
-    return (wide * inv_rms * gain.astype(F32)).astype(BF16)
 
 
 def attn_kernel(sp_size, pos_ref, freq_ref, tok_hbm, gain_hbm, wq_hbm, wk_hbm, wv_hbm, ck_hbm, cv_hbm,
@@ -177,6 +171,228 @@
 VMEM_A = 67043328 - (448 << 10)
 
 
+def partner(index, k):
+    if k == 0:
+        return index
+    if k == 1:
+        return index + 1 - 2 * lax.rem(index, 2)
+    if k == 2:
+        return lax.rem(index + 2, 4)
+    return 3 - index
+
+
+def finish_kernel(part_ref, tok_hbm, gain_hbm, wo_hbm, wg_hbm, wu_hbm, wd_hbm, out_ref,
+                  wo, wg, wu, wd, tokv, gain, r1, y2, r2, r3, y4, r4, fin,
+                  sem_w, s1, g1, s2, g2, s3, g3, s4, g4, s5z, g5z, s5y, g5y, s5c, g5c):
+    s = lax.axis_index("sp")
+    z = lax.axis_index("tp")
+    width = wo.shape[1]
+    wide = width // 2
+    dim = part_ref.shape[2] - 128
+    own_rows = part_ref.shape[1] // 2
+
+    loads = [pltpu.make_async_copy(src, dst, sem_w.at[i]) for i, (src, dst) in enumerate((
+        (tok_hbm.at[pl.ds(pl.multiple_of(s * own_rows, own_rows), own_rows)], tokv), (gain_hbm, gain),
+        (wo_hbm, wo), (wg_hbm, wg), (wu_hbm, wu), (wd_hbm, wd)))]
+    for copy in loads:
+        copy.start()
+
+    barrier = pltpu.get_barrier_semaphore()
+    for k in (1, 2, 3):
+        pl.semaphore_signal(barrier, inc=1, device_id={"tp": partner(z, k)}, device_id_type=MESH)
+        pl.semaphore_signal(barrier, inc=1, device_id={"sp": partner(s, k)}, device_id_type=MESH)
+    pl.semaphore_wait(barrier, 6)
+
+    def send(src, dst, send_sem, recv_sem, **target):
+        copy = pltpu.make_async_remote_copy(src_ref=src, dst_ref=dst, send_sem=send_sem, recv_sem=recv_sem,
+                                            device_id=target, device_id_type=MESH)
+        copy.start()
+        return copy
+
+    first = [send(part_ref.at[partner(s, k)], r1.at[k - 1], s1.at[k - 1], g1.at[k - 1], sp=partner(s, k)) for k in (3, 2, 1)]
+
+    sub = lax.broadcasted_iota(jnp.int32, (8, wide), 0)
+    low = sub < 4
+
+    def piece(left, right, d):
+        t = d // 2
+        a, b = left[8 * t:8 * t + 8], right[8 * t:8 * t + 8]
+        mask = low[:, :a.shape[1]]
+        return jnp.where(mask, a, b) if d % 2 == 0 else jnp.where(mask, b, a)
+
+    def swap(x):
+        return jnp.concatenate([pltpu.roll(x[8 * t:8 * t + 8], 4, 0) for t in range(x.shape[0] // 8)], axis=0)
+
+    def rows_of(four):
+        lefts, rights = [], []
+        for t in range(2):
+            a, b = four[2 * t], four[2 * t + 1]
+            mask = low[:, :a.shape[1]]
+            lefts.append(jnp.where(mask, a, b))
+            rights.append(pltpu.roll(jnp.where(mask, b, a), 4, 0))
+        return jnp.concatenate(lefts, axis=0), jnp.concatenate(rights, axis=0)
+
+    loads[0].wait()
+    loads[1].wait()
+    tok = tokv[...].astype(F32)
+    tok_l, tok_r = tok[:, :wide], swap(tok[:, wide:])
+    tok_piece = piece(tok_l, tok_r, 0)
+    for d in (1, 2, 3):
+        tok_piece = jnp.where(z == d, piece(tok_l, tok_r, d), tok_piece)
+    gain_row = gain[...].astype(F32).reshape(1, -1)
+    even = lax.rem(z, 2) == 0
+    gain_piece = jnp.where(jnp.where(even, sub, 7 - sub) < 4, gain_row[:, :wide], gain_row[:, wide:])
+
+    for copy in first:
+        copy.wait_recv()
+    parts = [part_ref[s], r1[0], r1[1], r1[2]]
+    tops = [p[:, dim:dim + 1] for p in parts]
+    sums = [p[:, dim + 64:dim + 65] for p in parts]
+    top = jnp.maximum(jnp.maximum(tops[0], tops[1]), jnp.maximum(tops[2], tops[3]))
+    scales = [jnp.exp(t - top) for t in tops]
+    total = sum(f * l for f, l in zip(scales, sums))
+    mixed = sum(f * p[:, :dim] for f, p in zip(scales, parts)) / total
+    att = jnp.concatenate([mixed[:own_rows], mixed[own_rows:]], axis=1)
+    att_swapped = swap(att).astype(BF16)
+    att = att.astype(BF16)
+
+    loads[2].wait()
+    second = []
+    for c, (at, size) in enumerate(CUT_O):
+        left = jnp.dot(att, wo[:, at:at + size], preferred_element_type=F32)
+        right = jnp.dot(att_swapped, wo[:, wide + at:wide + at + size], preferred_element_type=F32)
+        for d in range(4):
+            y2[d, :, at:at + size] = piece(left, right, d)
+        for k in (3, 2, 1):
+            second.append(send(y2.at[partner(z, k), :, pl.ds(at, size)], r2.at[k - 1, :, pl.ds(at, size)],
+                               s2.at[k - 1, c], g2.at[k - 1, c], tp=partner(z, k)))
+    for copy in second:
+        copy.wait_recv()
+    hidden = (tok_piece + (y2[z] + r2[0] + r2[1] + r2[2])).astype(BF16).astype(F32)
+    squares = jnp.sum(hidden * hidden, axis=-1, keepdims=True)
+    squares = jnp.broadcast_to(squares, (8, 128))
+    squares = squares + pltpu.roll(squares, 4, 0)
+    inv_rms = lax.rsqrt(squares[:, :1] / width + NORM_EPS)
+    r3[z] = (hidden * inv_rms * gain_piece).astype(BF16).astype(F32)
+
+    third = []
+    for c, (at, size) in enumerate(CUT_M):
+        for k in (3, 2, 1):
+            third.append(send(r3.at[z, :, pl.ds(at, size)], r3.at[z, :, pl.ds(at, size)], s3.at[k - 1, c], g3.at[k - 1, c],
+                              tp=partner(z, k)))
+    loads[3].wait()
+    loads[4].wait()
+    gate = up = None
+    for c, (at, size) in enumerate(CUT_M):
+        for copy in third[3 * c:3 * c + 3]:
+            copy.wait_recv()
+        left, right = rows_of([r3[d, :, at:at + size] for d in range(4)])
+        left, right = left.astype(BF16), right.astype(BF16)
+        pair = []
+        for w in (wg, wu):
+            pair.append(jnp.dot(left, w[at:at + size, :], preferred_element_type=F32)
+                        + jnp.dot(right, w[wide + at:wide + at + size, :], preferred_element_type=F32))
+        gate = pair[0] if gate is None else gate + pair[0]
+        up = pair[1] if up is None else up + pair[1]
+    act = gate * (1.0 / (1.0 + jnp.exp(-gate))) * up
+    act = act.astype(BF16)
+    act_swapped = swap(act.astype(F32)).astype(BF16)
+
+    loads[5].wait()
+    fourth = []
+    for c, (at, size) in enumerate(CUT_D):
+        left = jnp.dot(act, wd[:, at:at + size], preferred_element_type=F32)
+        right = jnp.dot(act_swapped, wd[:, wide + at:wide + at + size], preferred_element_type=F32)
+        for d in range(4):
+            y4[d, :, at:at + size] = piece(left, right, d)
+        for k in (3, 2, 1):
+            fourth.append(send(y4.at[partner(z, k), :, pl.ds(at, size)], r4.at[k - 1, :, pl.ds(at, size)],
+                               s4.at[k - 1, c], g4.at[k - 1, c], tp=partner(z, k)))
+
+    along, across, beside = {}, {}, {}
+    for c, (at, size) in enumerate(CUT_D):
+        for copy in fourth[3 * c:3 * c + 3]:
+            copy.wait_recv()
+        span = pl.ds(at, size)
+        total = y4[z, :, at:at + size] + r4[0, :, at:at + size] + r4[1, :, at:at + size] + r4[2, :, at:at + size]
+        fin[s, z, :, at:at + size] = (hidden[:, at:at + size] + total).astype(BF16).astype(F32)
+        mine = fin.at[s, z, :, span]
+        for k in (3, 2, 1):
+            along[c, k] = send(mine, mine, s5z.at[k - 1, c], g5z.at[k - 1, c], tp=partner(z, k))
+        across[c, 0] = send(mine, mine, s5y.at[0, c], g5y.at[0, c], sp=partner(s, 2))
+        beside[c, 0] = send(mine, mine, s5c.at[0, c], g5c.at[0, c], sp=partner(s, 1))
+    for c, (at, size) in enumerate(CUT_D):
+        span = pl.ds(at, size)
+        for k in range(4):
+            if k:
+                along[c, k].wait_recv()
+                came = fin.at[s, partner(z, k), :, span]
+                across[c, k] = send(came, came, s5y.at[k, c], g5y.at[k, c], sp=partner(s, 2))
+                beside[c, k] = send(came, came, s5c.at[k, c], g5c.at[k, c], sp=partner(s, 1))
+        for k in range(4):
+            across[c, k].wait_recv()
+            came = fin.at[partner(s, 2), partner(z, k), :, span]
+            beside[c, 4 + k] = send(came, came, s5c.at[4 + k, c], g5c.at[4 + k, c], sp=partner(s, 1))
+    for copy in beside.values():
+        copy.wait_recv()
+    for r in range(4):
+        left, right = rows_of([fin[r, d] for d in range(4)])
+        out_ref[pl.ds(own_rows * r, own_rows), 0:wide] = left.astype(BF16)
+        out_ref[pl.ds(own_rows * r, own_rows), wide:width] = right.astype(BF16)
+    for copy in first + second + third + fourth + list(along.values()) + list(across.values()) + list(beside.values()):
+        copy.wait_send()
+
+
+MESH = pl.DeviceIdType.MESH
+CUT_O = ((0, 512), (512, 768))
+CUT_M = ((0, 768), (768, 512))
+CUT_D = ((0, 512), (512, 768))
+
+
+def finish(part, tokens, gain, w_o, w_gate, w_up, w_down):
+    rows, width = tokens.shape
+    hbm = pl.BlockSpec(memory_space=pltpu.HBM)
+    vmem = pl.BlockSpec(memory_space=pltpu.VMEM)
+    own = part.shape[1] // 2
+    half = width // 2
+    dma = pltpu.SemaphoreType.DMA
+    return pl.pallas_call(
+        finish_kernel,
+        name="finish",
+        out_shape=jax.ShapeDtypeStruct((rows, width), BF16),
+        in_specs=[vmem] + [hbm] * 6,
+        out_specs=vmem,
+        scratch_shapes=[
+            pltpu.VMEM(w_o.shape, BF16),
+            pltpu.VMEM(w_gate.shape, BF16),
+            pltpu.VMEM(w_up.shape, BF16),
+            pltpu.VMEM(w_down.shape, BF16),
+            pltpu.VMEM((own, width), BF16),
+            pltpu.VMEM((width,), BF16),
+            pltpu.VMEM((3,) + part.shape[1:], F32),
+            pltpu.VMEM((4, 8, half), F32),
+            pltpu.VMEM((3, 8, half), F32),
+            pltpu.VMEM((4, 8, half), F32),
+            pltpu.VMEM((4, 8, half), F32),
+            pltpu.VMEM((3, 8, half), F32),
+            pltpu.VMEM((4, 4, 8, half), F32),
+            dma((6,)),
+            dma((3,)), dma((3,)),
+            dma((3, len(CUT_O))), dma((3, len(CUT_O))),
+            dma((3, len(CUT_M))), dma((3, len(CUT_M))),
+            dma((3, len(CUT_D))), dma((3, len(CUT_D))),
+            dma((3, len(CUT_D))), dma((3, len(CUT_D))),
+            dma((4, len(CUT_D))), dma((4, len(CUT_D))),
+            dma((8, len(CUT_D))), dma((8, len(CUT_D))),
+        ],
+        compiler_params=pltpu.CompilerParams(collective_id=0, has_side_effects=True, vmem_limit_bytes=VMEM_B),
+        cost_estimate=pl.CostEstimate(flops=2 * 16 * width * 2560 * 3, bytes_accessed=42 << 20, transcendentals=0),
+    )(part, tokens, gain, w_o, w_gate, w_up, w_down)
+
+
+VMEM_B = 62 << 20
+
+
 def solution(mesh):
     sp_size = mesh.shape["sp"]
     cache_spec = P("dp", "sp", "tp", None)
@@ -186,23 +402,8 @@
     out_specs = (row_spec, cache_spec, cache_spec)
 
     def local_step(tokens, positions, cache_k, cache_v, attn_gain, w_q, w_k, w_v, w_o, mlp_gain, w_gate, w_up, w_down):
-        rows = tokens.shape[0]
-        dim = cache_k.shape[3]
         new_k, new_v, part = attend(tokens, positions, cache_k, cache_v, attn_gain, w_q, w_k, w_v, sp_size)
-        o = part[:, :, :dim]; m = part[:, :, dim:dim + 1]; l = part[:, :, dim + 64:dim + 65]
-        gm = lax.pmax(m, "sp")
-        f = jnp.exp(m - gm)
-        tot = lax.psum(jnp.concatenate([o * f, l * f], axis=-1), "sp")
-        att = (tot[..., :dim] / tot[..., dim:]).astype(BF16)
-        att = att.reshape(4, 2, 16, dim).transpose(0, 2, 1, 3).reshape(rows, 2 * dim)
-        attn_proj = lax.psum(jnp.dot(att, w_o, preferred_element_type=F32), "tp")
-        hidden = (tokens.astype(F32) + attn_proj).astype(BF16)
-        normed_mlp = rms_norm(hidden, mlp_gain)
-        gate_proj = jnp.dot(normed_mlp, w_gate, preferred_element_type=F32)
-        up_proj = jnp.dot(normed_mlp, w_up, preferred_element_type=F32)
-        activated = (jax.nn.silu(gate_proj) * up_proj).astype(BF16)
-        mlp_down = lax.psum(jnp.dot(activated, w_down, preferred_element_type=F32), "tp")
-        layer_out = (hidden.astype(F32) + mlp_down).astype(BF16)
+        layer_out = finish(part, tokens, mlp_gain, w_o, w_gate, w_up, w_down)
         return layer_out, new_k, new_v
 
     return jax.shard_map(local_step, mesh=mesh, in_specs=in_specs, out_specs=out_specs, check_vma=False)

time: 190 us -> 56.8 us (0.30)
  waiting for transfers between devices: 114 us -> 0 us
  Pallas kernels: 14.9 us -> 54.3 us
  matrix products: 24.4 us -> 0 us
  blocking collectives: 13.5 us -> 0 us
  between operations: 13.9 us -> 0.65 us
  other arithmetic: 6.87 us -> 0 us
    psum x3 -> x0, waiting for transfers between devices: 114 us -> none  [the longest x1 40.8 us: local_step(): attn_proj = lax.psum(jnp.dot(att, w_o, preferred_element_type=F32), 'tp')]
    pallas_call x0 -> x1, Pallas kernels: none -> 39.5 us  [finish(): pl.pallas_call(finish_kernel, name='finish', out_shape=jax.ShapeDtypeStru...]
    dot_general x3 -> x0, matrix products: 24.4 us -> none  [the longest x1 14.1 us: local_step(): jnp.dot(activated, w_down, preferred_element_type=F32)]
    pmax x1 -> x0, blocking collectives: 13.5 us -> none  [local_step(): gm = lax.pmax(m, 'sp')]
    convert_element_type x3 -> x0, other arithmetic: 2.87 us -> none  [the longest x1 1.87 us: local_step(): layer_out = (hidden.astype(F32) + mlp_down).astype(BF16)]
  transfers between devices with their start and end apart: 3 -> 0, of which waited for: 3 -> 0; matrix products, arithmetic and copies ran while one was open for 0% -> 0% of each run, Pallas kernels for 0% -> 0%
where the time goes in v2:
time: 56.8 us; the launch traced here: 56.6 us
  Pallas kernels  54.3 us (96%)
  local copies, waits for them, and re-layouts  1.72 us (3%)
  between operations  0.65 us (1%)
    pallas_call x1, Pallas kernels, finish(): pl.pallas_call(finish_kernel, name='finish', out_shape=jax.ShapeDtypeStru...  39.5 us
    pallas_call x1, Pallas kernels, attend(): pl.pallas_call(functools.partial(attn_kernel, sp_size), name='attend', ou...  14.8 us
    unnamed x1, local copies, waits for them, and re-layouts  1.72 us

profile of v2, /device:TPU:0, one launch (start us, length us, event | category | flops | bytes accessed | tf_op | source)
XLA Modules:
  0.0 56.6 jit_solution(11891831733313547819)
XLA Ops:
  0.6 14.8 %attend.1 = (bf16[64,256,256]{2,1,0:T(8,128)(2,1)}, bf16[64,256,256]{2,1,0:T(8,128)(2,1)}, f32[4,32,384]{2,1,0:T(8,128)}) custom-call(s32[64]{0:T(128)} %pos_ref.1, f32[1,128]{1,0:T(1,128)} %constant.5.freq_ref, bf16[64,2560]{1,0:T(8,128)(2,1)} %tok_hbm.3, bf16[2560]{0:T(1024)(128)(2,1)} %gain_hbm.2, bf16[2560,512]{1,0:T(8,128)(2,1)} %wq_hbm.1, ...), custom_call_target="tpu_custom_call" | custom-call | flops 335544320 | bytes 23068672 | tf_op jit(solution)/shard_map/attend/pallas_call | solution.py:137
  15.4 39.5 %finish.1 = bf16[64,2560]{1,0:T(8,128)(2,1)} custom-call(f32[4,32,384]{2,1,0:T(8,128)} %get-tuple-element.6.part_ref, bf16[64,2560]{1,0:T(8,128)(2,1)} %tok_hbm.3, bf16[2560]{0:T(1024)(128)(2,1)} %gain_hbm.3, bf16[512,2560]{1,0:T(8,128)(2,1)} %wo_hbm.1, bf16[2560,2560]{1,0:T(8,128)(2,1)} %wg_hbm.1, bf16[2560,2560]{1,0:T(8,128)(2,1)} %wu_hbm.1, ...), custom_call_target="tpu_custom_call" | custom-call | flops 629145600 | bytes 44040192 | tf_op jit(solution)/shard_map/finish/pallas_call | solution.py:359
  54.9 1.7 %copy.20 = bf16[64,2560]{1,0:T(8,128)(2,1)} copy(bf16[64,2560]{1,0:T(8,128)(2,1)} %finish.1) | data formatting | bytes 655360

commit v3 on v2

--- a/solution.py
+++ b/solution.py
@@ -16,8 +16,8 @@
 CHUNK = 16
 
 
-def attn_kernel(sp_size, pos_ref, freq_ref, tok_hbm, gain_hbm, wq_hbm, wk_hbm, wv_hbm, ck_hbm, cv_hbm,
-                nk_hbm, nv_hbm, part_ref, nk_ref, nv_ref, tok, gain, wq, wk, wv, qs, knew, vnew, posm,
+def attn_kernel(sp_size, pos_hbm, freq_hbm, tok_hbm, gain_hbm, wq_hbm, wk_hbm, wv_hbm, ck_hbm, cv_hbm,
+                nk_hbm, nv_hbm, part_ref, pos_ref, freq_ref, nk_ref, nv_ref, tok, gain, wq, wk, wv, qs, knew, vnew, posm,
                 sem_w, sem_k, sem_v, sem_ko, sem_vo):
     rows = tok.shape[0]
     local_slots = nk_ref.shape[1]
@@ -28,9 +28,9 @@
     base = lax.axis_index("sp") * local_slots
 
     loads = [pltpu.make_async_copy(src, dst, sem_w.at[i]) for i, (src, dst) in enumerate(
-        ((tok_hbm, tok), (gain_hbm, gain), (wk_hbm, wk), (wv_hbm, wv), (wq_hbm, wq)))]
-    for copy in loads:
-        copy.start()
+        ((tok_hbm, tok), (gain_hbm, gain), (wk_hbm, wk), (wv_hbm, wv), (wq_hbm, wq), (pos_hbm, pos_ref), (freq_hbm, freq_ref)))]
+    for i in (5, 6, 0, 1, 2, 3, 4):
+        loads[i].start()
     k_loads, v_loads, k_stores, v_stores = [], [], [], []
     for c in range(chunks):
         span = pl.ds(c * CHUNK, CHUNK)
@@ -38,9 +38,9 @@
         v_loads.append(pltpu.make_async_copy(cv_hbm.at[span], nv_ref.at[span], sem_v.at[c]))
         k_stores.append(pltpu.make_async_copy(nk_ref.at[span], nk_hbm.at[span], sem_ko.at[c]))
         v_stores.append(pltpu.make_async_copy(nv_ref.at[span], nv_hbm.at[span], sem_vo.at[c]))
-        k_loads[c].start()
-        v_loads[c].start()
-
+
+    loads[5].wait()
+    loads[6].wait()
     sub = lax.broadcasted_iota(jnp.int32, (8, 128), 0)
     for g in range(rows // 8):
         acc = jnp.zeros((8, 128), jnp.int32)
@@ -57,15 +57,22 @@
     inv_rms = lax.rsqrt(jnp.mean(wide * wide, axis=-1, keepdims=True) + NORM_EPS)
     normed = (wide * inv_rms * gain[...].astype(F32).reshape(1, -1)).astype(BF16)
 
+    def fetch(c):
+        if c < chunks:
+            k_loads[c].start()
+            v_loads[c].start()
+
     def rope(lin):
         a, b = lin[:, :half], lin[:, half:]
         return jnp.concatenate([a * cos - b * sin, b * cos + a * sin], axis=-1)
 
     loads[2].wait()
+    fetch(0)
     knew[...] = rope(jnp.dot(normed, wk[...], preferred_element_type=F32)).astype(BF16).astype(F32)
     loads[3].wait()
     vnew[...] = jnp.dot(normed, wv[...], preferred_element_type=F32).astype(BF16).astype(F32)
     loads[4].wait()
+    fetch(1)
     heads = wq.shape[1] // dim
     q_lin = jnp.dot(normed, wq[...], preferred_element_type=F32)
     q_rot = [rope(q_lin[:, h * dim:(h + 1) * dim]) for h in range(heads)]
@@ -85,6 +92,7 @@
     for c in range(chunks):
         offsets = [jnp.bitwise_and(pos_ref[c * CHUNK + j], slots - 1) - base for j in range(CHUNK)]
         k_loads[c].wait()
+        fetch(c + 2)
         for j in range(CHUNK):
             patch(nk_ref, knew, c * CHUNK + j, offsets[j])
         k_stores[c].start()
@@ -124,6 +132,10 @@
         copy.wait()
 
 
+def in_hbm(*arrays):
+    return [pltpu.with_memory_space_constraint(x, pltpu.HBM) for x in arrays]
+
+
 def attend(tokens, positions, cache_k, cache_v, gain, w_q, w_k, w_v, sp_size):
     rows, width = tokens.shape
     _, local_slots, _, dim = cache_k.shape
@@ -140,11 +152,13 @@
         out_shape=(
             jax.ShapeDtypeStruct((rows, local_slots, dim), BF16),
             jax.ShapeDtypeStruct((rows, local_slots, dim), BF16),
-            jax.ShapeDtypeStruct((sp_size, heads * rows // sp_size, dim + 128), F32),
+            pltpu.VMEM((sp_size, heads * rows // sp_size, dim + 128), F32),
         ),
-        in_specs=[pl.BlockSpec(memory_space=pltpu.SMEM), vmem_spec] + [any_spec] * 7,
+        in_specs=[any_spec] * 9,
         out_specs=[any_spec, any_spec, vmem_spec],
         scratch_shapes=[
+            pltpu.SMEM((rows,), jnp.int32),
+            pltpu.VMEM((1, dim // 2), F32),
             pltpu.VMEM((rows, local_slots, dim), BF16),
             pltpu.VMEM((rows, local_slots, dim), BF16),
             pltpu.VMEM((rows, width), BF16),
@@ -156,7 +170,7 @@
             pltpu.VMEM((rows, dim), F32),
             pltpu.VMEM((rows, dim), F32),
             pltpu.VMEM((rows, 128), jnp.int32),
-            pltpu.SemaphoreType.DMA((5,)),
+            pltpu.SemaphoreType.DMA((7,)),
             pltpu.SemaphoreType.DMA((chunks,)),
             pltpu.SemaphoreType.DMA((chunks,)),
             pltpu.SemaphoreType.DMA((chunks,)),
@@ -164,11 +178,11 @@
         ],
         compiler_params=pltpu.CompilerParams(vmem_limit_bytes=VMEM_A),
         cost_estimate=pl.CostEstimate(flops=2 * rows * width * 1024, bytes_accessed=22 << 20, transcendentals=0),
-    )(positions, jnp.asarray(freq).reshape(1, -1), tokens, gain, w_q, w_k, w_v, ck, cv)
+    )(*in_hbm(positions, jnp.asarray(freq).reshape(1, -1), tokens, gain, w_q, w_k, w_v, ck, cv))
     return nk.reshape(cache_k.shape), nv.reshape(cache_v.shape), part
 
 
-VMEM_A = 67043328 - (448 << 10)
+VMEM_A = 48 << 20
 
 
 def partner(index, k):
@@ -323,12 +337,13 @@
         beside[c, 0] = send(mine, mine, s5c.at[0, c], g5c.at[0, c], sp=partner(s, 1))
     for c, (at, size) in enumerate(CUT_D):
         span = pl.ds(at, size)
-        for k in range(4):
-            if k:
-                along[c, k].wait_recv()
-                came = fin.at[s, partner(z, k), :, span]
-                across[c, k] = send(came, came, s5y.at[k, c], g5y.at[k, c], sp=partner(s, 2))
-                beside[c, k] = send(came, came, s5c.at[k, c], g5c.at[k, c], sp=partner(s, 1))
+        for k in (1, 2, 3):
+            along[c, k].wait_recv()
+            came = fin.at[s, partner(z, k), :, span]
+            across[c, k] = send(came, came, s5y.at[k, c], g5y.at[k, c], sp=partner(s, 2))
+            beside[c, k] = send(came, came, s5c.at[k, c], g5c.at[k, c], sp=partner(s, 1))
+    for c, (at, size) in enumerate(CUT_D):
+        span = pl.ds(at, size)
         for k in range(4):
             across[c, k].wait_recv()
             came = fin.at[partner(s, 2), partner(z, k), :, span]
@@ -344,9 +359,9 @@
 
 
 MESH = pl.DeviceIdType.MESH
-CUT_O = ((0, 512), (512, 768))
-CUT_M = ((0, 768), (768, 512))
-CUT_D = ((0, 512), (512, 768))
+CUT_O = ((0, 256), (256, 1024))
+CUT_M = ((0, 256), (256, 512), (768, 512))
+CUT_D = ((0, 256), (256, 512), (768, 512))
 
 
 def finish(part, tokens, gain, w_o, w_gate, w_up, w_down):
@@ -359,7 +374,7 @@
     return pl.pallas_call(
         finish_kernel,
         name="finish",
-        out_shape=jax.ShapeDtypeStruct((rows, width), BF16),
+        out_shape=pltpu.VMEM((rows, width), BF16),
         in_specs=[vmem] + [hbm] * 6,
         out_specs=vmem,
         scratch_shapes=[
@@ -387,10 +402,10 @@
         ],
         compiler_params=pltpu.CompilerParams(collective_id=0, has_side_effects=True, vmem_limit_bytes=VMEM_B),
         cost_estimate=pl.CostEstimate(flops=2 * 16 * width * 2560 * 3, bytes_accessed=42 << 20, transcendentals=0),
-    )(part, tokens, gain, w_o, w_gate, w_up, w_down)
-
-
-VMEM_B = 62 << 20
+    )(part, *in_hbm(tokens, gain, w_o, w_gate, w_up, w_down))
+
+
+VMEM_B = 48 << 20
 
 
 def solution(mesh):

time: 56.8 us -> 51.7 us (0.910)
  Pallas kernels: 54.3 us -> 50.2 us
  local copies, waits for them, and re-layouts: 1.72 us -> 0.73 us
    pallas_call x1, Pallas kernels: 39.5 us -> 36.3 us  [finish(): pl.pallas_call(finish_kernel, name='finish', out_shape=pltpu.VMEM((rows,...]
    unnamed x1, local copies, waits for them, and re-layouts: 1.72 us -> 0.73 us
    pallas_call x1, Pallas kernels: 14.8 us -> 13.8 us  [attend(): pl.pallas_call(functools.partial(attn_kernel, sp_size), name='attend', ou...]
where the time goes in v3:
time: 51.7 us; the launch traced here: 51.5 us
  Pallas kernels  50.2 us (97%)
  local copies, waits for them, and re-layouts  0.73 us (1%)
  between operations  0.65 us (1%)
    pallas_call x1, Pallas kernels, finish(): pl.pallas_call(finish_kernel, name='finish', out_shape=pltpu.VMEM((rows,...  36.3 us
    pallas_call x1, Pallas kernels, attend(): pl.pallas_call(functools.partial(attn_kernel, sp_size), name='attend', ou...  13.8 us

profile of v3, /device:TPU:0, one launch (start us, length us, event | category | flops | bytes accessed | tf_op | source)
XLA Modules:
  0.0 51.5 jit_solution(14926299899581681007)
XLA Ops:
  0.6 13.8 %attend.1 = (bf16[64,256,256]{2,1,0:T(8,128)(2,1)}, bf16[64,256,256]{2,1,0:T(8,128)(2,1)}, f32[4,32,384]{2,1,0:T(8,128)S(1)}) custom-call(s32[64]{0:T(128)} %pos_hbm.1, f32[1,128]{1,0:T(1,128)} %constant.5.freq_hbm, bf16[64,2560]{1,0:T(8,128)(2,1)} %tok_hbm.3, bf16[2560]{0:T(1024)(128)(2,1)} %gain_hbm.2, bf16[2560,512]{1,0:T(8,128)(2,1)} %wq_hbm.1, ...), custom_call_target="tpu_custom_call" | custom-call | flops 335544320 | bytes 23068672 | tf_op jit(solution)/shard_map/attend/pallas_call | solution.py:149
  14.5 36.3 %finish.1 = bf16[64,2560]{1,0:T(8,128)(2,1)S(1)} custom-call(f32[4,32,384]{2,1,0:T(8,128)S(1)} %get-tuple-element.6.part_ref, bf16[64,2560]{1,0:T(8,128)(2,1)} %tok_hbm.3, bf16[2560]{0:T(1024)(128)(2,1)} %gain_hbm.3, bf16[512,2560]{1,0:T(8,128)(2,1)} %wo_hbm.1, bf16[2560,2560]{1,0:T(8,128)(2,1)} %wg_hbm.1, bf16[2560,2560]{1,0:T(8,128)(2,1)} %wu_hbm.1, ...), custom_call_target="tpu_custom_call" | custom-call | flops 629145600 | bytes 44040192 | tf_op jit(solution)/shard_map/finish/pallas_call | solution.py:374
  50.8 0.7 %copy.20 = bf16[64,2560]{1,0:T(8,128)(2,1)} copy(bf16[64,2560]{1,0:T(8,128)(2,1)S(1)} %finish.1) | data formatting | bytes 655360

commit v4 on v1

--- a/solution.py
+++ b/solution.py
@@ -16,14 +16,8 @@
 CHUNK = 16
 
 
-def rms_norm(values, gain):
-    wide = values.astype(F32)
-    inv_rms = lax.rsqrt(jnp.mean(wide * wide, axis=-1, keepdims=True) + NORM_EPS)
-    return (wide * inv_rms * gain.astype(F32)).astype(BF16)
-
-
-def attn_kernel(sp_size, pos_ref, freq_ref, tok_hbm, gain_hbm, wq_hbm, wk_hbm, wv_hbm, ck_hbm, cv_hbm,
-                nk_hbm, nv_hbm, part_ref, nk_ref, nv_ref, tok, gain, wq, wk, wv, qs, knew, vnew, posm,
+def attn_kernel(sp_size, pos_hbm, freq_hbm, tok_hbm, gain_hbm, wq_hbm, wk_hbm, wv_hbm, ck_hbm, cv_hbm,
+                nk_hbm, nv_hbm, part_ref, pos_ref, freq_ref, nk_ref, nv_ref, tok, gain, wq, wk, wv, qs, knew, vnew, posm,
                 sem_w, sem_k, sem_v, sem_ko, sem_vo):
     rows = tok.shape[0]
     local_slots = nk_ref.shape[1]
@@ -34,9 +28,9 @@
     base = lax.axis_index("sp") * local_slots
 
     loads = [pltpu.make_async_copy(src, dst, sem_w.at[i]) for i, (src, dst) in enumerate(
-        ((tok_hbm, tok), (gain_hbm, gain), (wk_hbm, wk), (wv_hbm, wv), (wq_hbm, wq)))]
-    for copy in loads:
-        copy.start()
+        ((tok_hbm, tok), (gain_hbm, gain), (wk_hbm, wk), (wv_hbm, wv), (wq_hbm, wq), (pos_hbm, pos_ref), (freq_hbm, freq_ref)))]
+    for i in (5, 6, 0, 1, 2, 3, 4):
+        loads[i].start()
     k_loads, v_loads, k_stores, v_stores = [], [], [], []
     for c in range(chunks):
         span = pl.ds(c * CHUNK, CHUNK)
@@ -44,9 +38,9 @@
         v_loads.append(pltpu.make_async_copy(cv_hbm.at[span], nv_ref.at[span], sem_v.at[c]))
         k_stores.append(pltpu.make_async_copy(nk_ref.at[span], nk_hbm.at[span], sem_ko.at[c]))
         v_stores.append(pltpu.make_async_copy(nv_ref.at[span], nv_hbm.at[span], sem_vo.at[c]))
-        k_loads[c].start()
-        v_loads[c].start()
-
+
+    loads[5].wait()
+    loads[6].wait()
     sub = lax.broadcasted_iota(jnp.int32, (8, 128), 0)
     for g in range(rows // 8):
         acc = jnp.zeros((8, 128), jnp.int32)
@@ -63,15 +57,22 @@
     inv_rms = lax.rsqrt(jnp.mean(wide * wide, axis=-1, keepdims=True) + NORM_EPS)
     normed = (wide * inv_rms * gain[...].astype(F32).reshape(1, -1)).astype(BF16)
 
+    def fetch(c):
+        if c < chunks:
+            k_loads[c].start()
+            v_loads[c].start()
+
     def rope(lin):
         a, b = lin[:, :half], lin[:, half:]
         return jnp.concatenate([a * cos - b * sin, b * cos + a * sin], axis=-1)
 
     loads[2].wait()
+    fetch(0)
     knew[...] = rope(jnp.dot(normed, wk[...], preferred_element_type=F32)).astype(BF16).astype(F32)
     loads[3].wait()
     vnew[...] = jnp.dot(normed, wv[...], preferred_element_type=F32).astype(BF16).astype(F32)
     loads[4].wait()
+    fetch(1)
     heads = wq.shape[1] // dim
     q_lin = jnp.dot(normed, wq[...], preferred_element_type=F32)
     q_rot = [rope(q_lin[:, h * dim:(h + 1) * dim]) for h in range(heads)]
@@ -91,6 +92,7 @@
     for c in range(chunks):
         offsets = [jnp.bitwise_and(pos_ref[c * CHUNK + j], slots - 1) - base for j in range(CHUNK)]
         k_loads[c].wait()
+        fetch(c + 2)
         for j in range(CHUNK):
             patch(nk_ref, knew, c * CHUNK + j, offsets[j])
         k_stores[c].start()
@@ -130,6 +132,10 @@
         copy.wait()
 
 
+def in_hbm(*arrays):
+    return [pltpu.with_memory_space_constraint(x, pltpu.HBM) for x in arrays]
+
+
 def attend(tokens, positions, cache_k, cache_v, gain, w_q, w_k, w_v, sp_size):
     rows, width = tokens.shape
     _, local_slots, _, dim = cache_k.shape
@@ -146,11 +152,13 @@
         out_shape=(
             jax.ShapeDtypeStruct((rows, local_slots, dim), BF16),
             jax.ShapeDtypeStruct((rows, local_slots, dim), BF16),
-            jax.ShapeDtypeStruct((sp_size, heads * rows // sp_size, dim + 128), F32),
+            pltpu.VMEM((sp_size, heads * rows // sp_size, dim + 128), F32),
         ),
-        in_specs=[pl.BlockSpec(memory_space=pltpu.SMEM), vmem_spec] + [any_spec] * 7,
+        in_specs=[any_spec] * 9,
         out_specs=[any_spec, any_spec, vmem_spec],
         scratch_shapes=[
+            pltpu.SMEM((rows,), jnp.int32),
+            pltpu.VMEM((1, dim // 2), F32),
             pltpu.VMEM((rows, local_slots, dim), BF16),
             pltpu.VMEM((rows, local_slots, dim), BF16),
             pltpu.VMEM((rows, width), BF16),
@@ -162,7 +170,7 @@
             pltpu.VMEM((rows, dim), F32),
             pltpu.VMEM((rows, dim), F32),
             pltpu.VMEM((rows, 128), jnp.int32),
-            pltpu.SemaphoreType.DMA((5,)),
+            pltpu.SemaphoreType.DMA((7,)),
             pltpu.SemaphoreType.DMA((chunks,)),
             pltpu.SemaphoreType.DMA((chunks,)),
             pltpu.SemaphoreType.DMA((chunks,)),
@@ -170,11 +178,291 @@
         ],
         compiler_params=pltpu.CompilerParams(vmem_limit_bytes=VMEM_A),
         cost_estimate=pl.CostEstimate(flops=2 * rows * width * 1024, bytes_accessed=22 << 20, transcendentals=0),
-    )(positions, jnp.asarray(freq).reshape(1, -1), tokens, gain, w_q, w_k, w_v, ck, cv)
+    )(*in_hbm(positions, jnp.asarray(freq).reshape(1, -1), tokens, gain, w_q, w_k, w_v, ck, cv))
     return nk.reshape(cache_k.shape), nv.reshape(cache_v.shape), part
 
 
-VMEM_A = 67043328 - (448 << 10)
+VMEM_A = 48 << 20
+
+
+def partner(index, k):
+    if k == 0:
+        return index
+    if k == 1:
+        return index + 1 - 2 * lax.rem(index, 2)
+    if k == 2:
+        return lax.rem(index + 2, 4)
+    return 3 - index
+
+
+def finish_kernel(part_ref, tok_hbm, gain_hbm, wo_hbm, wg_hbm, wu_hbm, wd_hbm, out_ref,
+                  wo, wg, wu, wd, tokv, gain, r1, y2, r2, hid, norm, ms, y4, r4, fin,
+                  sem_w, s1, g1, s2, g2, s3, g3, s4, g4, s5z, g5z, s5y, g5y, s5c, g5c):
+    s = lax.axis_index("sp")
+    z = lax.axis_index("tp")
+    line, core = s // 2, lax.rem(s, 2)
+    width = wo.shape[1]
+    dim = part_ref.shape[2] - 128
+    own_rows = part_ref.shape[1] // 2
+    owner = (core == 1) & ((z == 1) | (z == 2))
+    tile = jnp.clip(z - 1, 0, 1)
+
+    loads = [pltpu.make_async_copy(src, dst, sem_w.at[i]) for i, (src, dst) in enumerate((
+        (tok_hbm.at[pl.ds(pl.multiple_of(2 * line * own_rows, own_rows), 2 * own_rows)], tokv), (gain_hbm, gain),
+        (wo_hbm, wo), (wg_hbm, wg), (wu_hbm, wu), (wd_hbm, wd)))]
+    for copy in loads:
+        copy.start()
+
+    def is_owner(t):
+        return (core == 1) & (z == t + 1)
+
+    barrier = pltpu.get_barrier_semaphore()
+    for k in (1, 2, 3):
+        pl.semaphore_signal(barrier, inc=1, device_id={"sp": partner(s, k), "tp": z}, device_id_type=MESH)
+    for t in range(2):
+        @pl.when(z != t + 1)
+        def _():
+            pl.semaphore_signal(barrier, inc=1, device_id={"sp": 2 * line + 1, "tp": t + 1}, device_id_type=MESH)
+
+    @pl.when(owner)
+    def _():
+        for k in (1, 2, 3):
+            pl.semaphore_signal(barrier, inc=1, device_id={"sp": 2 * line, "tp": partner(z, k)}, device_id_type=MESH)
+        for k in (1, 2):
+            pl.semaphore_signal(barrier, inc=1, device_id={"sp": 2 * line + 1, "tp": partner(z, k)}, device_id_type=MESH)
+
+    middle = (z == 1) | (z == 2)
+    pl.semaphore_wait(barrier, jnp.where(middle, jnp.where(core == 1, 9, 4), 5))
+
+    def remote(src, dst, send_sem, recv_sem, sp, tp):
+        return pltpu.make_async_remote_copy(src_ref=src, dst_ref=dst, send_sem=send_sem, recv_sem=recv_sem,
+                                            device_id={"sp": sp, "tp": tp}, device_id_type=MESH)
+
+    first = [remote(part_ref.at[partner(s, k)], r1.at[k - 1], s1.at[k - 1], g1.at[k - 1], partner(s, k), z) for k in (3, 2, 1)]
+    for copy in first:
+        copy.start()
+
+    def to_owner(t, c, cut, rows, sums, send_sem, recv_sem):
+        span = pl.ds(*cut[c])
+        return remote(rows.at[t, :, span], sums.at[core, z, :, span], send_sem.at[t, c], recv_sem.at[core, z, c], 2 * line + 1, t + 1)
+
+    def send_sums(value, c, cut, rows, sums, send_sem, recv_sem):
+        at, size = cut[c]
+        for t in range(2):
+            rows[t, :, at:at + size] = value[8 * t:8 * t + 8]
+        for t in range(2):
+            @pl.when(jnp.logical_not(is_owner(t)))
+            def _():
+                to_owner(t, c, cut, rows, sums, send_sem, recv_sem).start()
+
+    def wait_sums(c, cut, rows, sums, send_sem, recv_sem):
+        at, size = cut[c]
+        span = pl.ds(at, size)
+        sums[1, z, :, at:at + size] = rows[tile, :, at:at + size]
+        for b in range(2):
+            for k in (1, 3, 2, 0):
+                if b == 0 or k:
+                    far = partner(z, k)
+                    remote(rows.at[0, :, span], sums.at[b, far, :, span], send_sem.at[0, c], recv_sem.at[b, far, c], 2 * line + b, far).wait_recv()
+        return [sums[b, 0, :, at:at + size] + sums[b, 1, :, at:at + size] + sums[b, 2, :, at:at + size] + sums[b, 3, :, at:at + size]
+                for b in range(2)]
+
+    def sent_sums(cut, rows, sums, send_sem, recv_sem):
+        for t in range(2):
+            @pl.when(jnp.logical_not(is_owner(t)))
+            def _():
+                for c in range(len(cut)):
+                    to_owner(t, c, cut, rows, sums, send_sem, recv_sem).wait_send()
+
+    for copy in first:
+        copy.wait_recv()
+    parts = [part_ref[s], r1[0], r1[1], r1[2]]
+    tops = [p[:, dim:dim + 1] for p in parts]
+    sums = [p[:, dim + 64:dim + 65] for p in parts]
+    top = jnp.maximum(jnp.maximum(tops[0], tops[1]), jnp.maximum(tops[2], tops[3]))
+    scales = [jnp.exp(t - top) for t in tops]
+    total = sum(f * l for f, l in zip(scales, sums))
+    mixed = sum(f * p[:, :dim] for f, p in zip(scales, parts)) / total
+    att = jnp.concatenate([mixed[:own_rows], mixed[own_rows:]], axis=1).astype(BF16)
+
+    loads[2].wait()
+    for c, (at, size) in enumerate(CUT_O):
+        send_sums(jnp.dot(att, wo[:, at:at + size], preferred_element_type=F32), c, CUT_O, y2, r2, s2, g2)
+
+    def spread(b, k, c):
+        span = pl.ds(*CUT_M[c])
+        return remote(norm.at[b, :, span], ms.at[tile, :, span], s3.at[b, k, c], g3.at[tile, c], 2 * line + b, partner(z, k))
+
+    loads[0].wait()
+    loads[1].wait()
+
+    @pl.when(owner)
+    def _():
+        halves = [wait_sums(c, CUT_O, y2, r2, s2, g2) for c in range(len(CUT_O))]
+        for b in range(2):
+            tok = tokv[pl.ds(own_rows * b, own_rows), :].astype(F32)
+            tok = jnp.where(tile == 0, tok[0:8], tok[8:16])
+            hidden = (tok + jnp.concatenate([h[b] for h in halves], axis=1)).astype(BF16).astype(F32)
+            inv_rms = lax.rsqrt(jnp.mean(hidden * hidden, axis=-1, keepdims=True) + NORM_EPS)
+            normed = (hidden * inv_rms * gain[...].astype(F32).reshape(1, -1)).astype(BF16).astype(F32)
+            hid[b] = hidden
+            norm[b] = normed
+            if b == 1:
+                ms[tile] = normed
+        for c in range(len(CUT_M)):
+            for k in (2, 3, 1, 0):
+                for b in (0, 1):
+                    if b == 0 or k:
+                        spread(b, k, c).start()
+
+    loads[3].wait()
+    loads[4].wait()
+    gate = up = None
+    for c, (at, size) in enumerate(CUT_M):
+        span = pl.ds(at, size)
+        for t in range(2):
+            @pl.when(jnp.logical_not(is_owner(t)))
+            def _():
+                remote(norm.at[0, :, span], ms.at[t, :, span], s3.at[0, 0, c], g3.at[t, c], 2 * line + 1, t + 1).wait_recv()
+        rows = jnp.concatenate([ms[0, :, at:at + size], ms[1, :, at:at + size]], axis=0).astype(BF16)
+        pair = [jnp.dot(rows, w[at:at + size, :], preferred_element_type=F32) for w in (wg, wu)]
+        gate = pair[0] if gate is None else gate + pair[0]
+        up = pair[1] if up is None else up + pair[1]
+    act = gate * (1.0 / (1.0 + jnp.exp(-gate))) * up
+    act = act.astype(BF16)
+
+    loads[5].wait()
+    for c, (at, size) in enumerate(CUT_D):
+        send_sums(jnp.dot(act, wd[:, at:at + size], preferred_element_type=F32), c, CUT_D, y4, r4, s4, g4)
+
+    def along(t, k, c):
+        span = pl.ds(*CUT_D[c])
+        rows = fin.at[line, t, :, :, span]
+        return remote(rows, rows, s5z.at[k, c], g5z.at[t, c], s, partner(z, k))
+
+    def across(t, c):
+        span = pl.ds(*CUT_D[c])
+        rows = fin.at[line, t, :, :, span]
+        return remote(rows, rows, s5y.at[t, c], g5y.at[t, c], partner(s, 2), z)
+
+    def beside(far, t, c):
+        span = pl.ds(*CUT_D[c])
+        rows = fin.at[line if far == 0 else 1 - line, t, :, :, span]
+        return remote(rows, rows, s5c.at[far, t, c], g5c.at[far, t, c], partner(s, 1), z)
+
+    @pl.when(owner)
+    def _():
+        for c, (at, size) in enumerate(CUT_D):
+            totals = wait_sums(c, CUT_D, y4, r4, s4, g4)
+            for b in range(2):
+                fin[line, tile, b, :, at:at + size] = (hid[b, :, at:at + size] + totals[b]).astype(BF16).astype(F32)
+            for k in (2, 3, 1):
+                along(tile, k, c).start()
+            across(tile, c).start()
+            beside(0, tile, c).start()
+
+    @pl.when(core == 1)
+    def _():
+        for c in range(len(CUT_D)):
+            for t in range(2):
+                @pl.when(z != t + 1)
+                def _():
+                    along(t, 1, c).wait_recv()
+                    across(t, c).start()
+                    beside(0, t, c).start()
+        for c in range(len(CUT_D)):
+            for t in range(2):
+                span = pl.ds(*CUT_D[c])
+                rows = fin.at[1 - line, t, :, :, span]
+                remote(rows, rows, s5y.at[t, c], g5y.at[t, c], partner(s, 2), z).wait_recv()
+                beside(1, t, c).start()
+
+    @pl.when(core == 0)
+    def _():
+        for far in range(2):
+            for c in range(len(CUT_D)):
+                for t in range(2):
+                    beside(far, t, c).wait_recv()
+
+    for y in range(2):
+        for b in range(2):
+            out_ref[pl.ds(own_rows * (2 * y + b), own_rows), :] = jnp.concatenate([fin[y, 0, b], fin[y, 1, b]], axis=0).astype(BF16)
+
+    for copy in first:
+        copy.wait_send()
+    sent_sums(CUT_O, y2, r2, s2, g2)
+    sent_sums(CUT_D, y4, r4, s4, g4)
+
+    @pl.when(owner)
+    def _():
+        for c in range(len(CUT_M)):
+            for k in range(4):
+                for b in range(2):
+                    if b == 0 or k:
+                        spread(b, k, c).wait_send()
+        for c in range(len(CUT_D)):
+            for k in (1, 2, 3):
+                along(tile, k, c).wait_send()
+
+    @pl.when(core == 1)
+    def _():
+        for c in range(len(CUT_D)):
+            for t in range(2):
+                across(t, c).wait_send()
+                beside(0, t, c).wait_send()
+                beside(1, t, c).wait_send()
+
+
+MESH = pl.DeviceIdType.MESH
+CUT_O = ((0, 512), (512, 2048))
+CUT_M = ((0, 512), (512, 512), (1024, 512), (1536, 512), (2048, 512))
+CUT_D = ((0, 512), (512, 512), (1024, 512), (1536, 512), (2048, 512))
+
+
+def finish(part, tokens, gain, w_o, w_gate, w_up, w_down):
+    rows, width = tokens.shape
+    hbm = pl.BlockSpec(memory_space=pltpu.HBM)
+    vmem = pl.BlockSpec(memory_space=pltpu.VMEM)
+    own = part.shape[1] // 2
+    dma = pltpu.SemaphoreType.DMA
+    cut_o, cut_m, cut_d = len(CUT_O), len(CUT_M), len(CUT_D)
+    return pl.pallas_call(
+        finish_kernel,
+        name="finish",
+        out_shape=pltpu.VMEM((rows, width), BF16),
+        in_specs=[vmem] + [hbm] * 6,
+        out_specs=vmem,
+        scratch_shapes=[
+            pltpu.VMEM(w_o.shape, BF16),
+            pltpu.VMEM(w_gate.shape, BF16),
+            pltpu.VMEM(w_up.shape, BF16),
+            pltpu.VMEM(w_down.shape, BF16),
+            pltpu.VMEM((2 * own, width), BF16),
+            pltpu.VMEM((width,), BF16),
+            pltpu.VMEM((3,) + part.shape[1:], F32),
+            pltpu.VMEM((2, 8, width), F32),
+            pltpu.VMEM((2, 4, 8, width), F32),
+            pltpu.VMEM((2, 8, width), F32),
+            pltpu.VMEM((2, 8, width), F32),
+            pltpu.VMEM((2, 8, width), F32),
+            pltpu.VMEM((2, 8, width), F32),
+            pltpu.VMEM((2, 4, 8, width), F32),
+            pltpu.VMEM((2, 2, 2, 8, width), F32),
+            dma((6,)),
+            dma((3,)), dma((3,)),
+            dma((2, cut_o)), dma((2, 4, cut_o)),
+            dma((2, 4, cut_m)), dma((2, cut_m)),
+            dma((2, cut_d)), dma((2, 4, cut_d)),
+            dma((4, cut_d)), dma((2, cut_d)),
+            dma((2, cut_d)), dma((2, cut_d)),
+            dma((2, 2, cut_d)), dma((2, 2, cut_d)),
+        ],
+        compiler_params=pltpu.CompilerParams(collective_id=0, has_side_effects=True, vmem_limit_bytes=VMEM_B),
+        cost_estimate=pl.CostEstimate(flops=2 * 16 * width * 2560 * 3, bytes_accessed=42 << 20, transcendentals=0),
+    )(part, *in_hbm(tokens, gain, w_o, w_gate, w_up, w_down))
+
+
+VMEM_B = 50 << 20
 
 
 def solution(mesh):
@@ -186,23 +474,8 @@
     out_specs = (row_spec, cache_spec, cache_spec)
 
     def local_step(tokens, positions, cache_k, cache_v, attn_gain, w_q, w_k, w_v, w_o, mlp_gain, w_gate, w_up, w_down):
-        rows = tokens.shape[0]
-        dim = cache_k.shape[3]
         new_k, new_v, part = attend(tokens, positions, cache_k, cache_v, attn_gain, w_q, w_k, w_v, sp_size)
-        o = part[:, :, :dim]; m = part[:, :, dim:dim + 1]; l = part[:, :, dim + 64:dim + 65]
-        gm = lax.pmax(m, "sp")
-        f = jnp.exp(m - gm)
-        tot = lax.psum(jnp.concatenate([o * f, l * f], axis=-1), "sp")
-        att = (tot[..., :dim] / tot[..., dim:]).astype(BF16)
-        att = att.reshape(4, 2, 16, dim).transpose(0, 2, 1, 3).reshape(rows, 2 * dim)
-        attn_proj = lax.psum(jnp.dot(att, w_o, preferred_element_type=F32), "tp")
-        hidden = (tokens.astype(F32) + attn_proj).astype(BF16)
-        normed_mlp = rms_norm(hidden, mlp_gain)
-        gate_proj = jnp.dot(normed_mlp, w_gate, preferred_element_type=F32)
-        up_proj = jnp.dot(normed_mlp, w_up, preferred_element_type=F32)
-        activated = (jax.nn.silu(gate_proj) * up_proj).astype(BF16)
-        mlp_down = lax.psum(jnp.dot(activated, w_down, preferred_element_type=F32), "tp")
-        layer_out = (hidden.astype(F32) + mlp_down).astype(BF16)
+        layer_out = finish(part, tokens, mlp_gain, w_o, w_gate, w_up, w_down)
         return layer_out, new_k, new_v
 
     return jax.shard_map(local_step, mesh=mesh, in_specs=in_specs, out_specs=out_specs, check_vma=False)

time: 190 us -> 50.4 us (0.27)
  waiting for transfers between devices: 114 us -> 0 us
  Pallas kernels: 14.9 us -> 48.8 us
  matrix products: 24.4 us -> 0 us
  blocking collectives: 13.5 us -> 0 us
  between operations: 13.9 us -> 0.65 us
  other arithmetic: 6.87 us -> 0 us
    psum x3 -> x0, waiting for transfers between devices: 114 us -> none  [the longest x1 40.8 us: local_step(): attn_proj = lax.psum(jnp.dot(att, w_o, preferred_element_type=F32), 'tp')]
    pallas_call x0 -> x1, Pallas kernels: none -> 35 us  [finish(): pl.pallas_call(finish_kernel, name='finish', out_shape=pltpu.VMEM((rows,...]
    dot_general x3 -> x0, matrix products: 24.4 us -> none  [the longest x1 14.1 us: local_step(): jnp.dot(activated, w_down, preferred_element_type=F32)]
    pmax x1 -> x0, blocking collectives: 13.5 us -> none  [local_step(): gm = lax.pmax(m, 'sp')]
    convert_element_type x3 -> x0, other arithmetic: 2.87 us -> none  [the longest x1 1.87 us: local_step(): layer_out = (hidden.astype(F32) + mlp_down).astype(BF16)]
  transfers between devices with their start and end apart: 3 -> 0, of which waited for: 3 -> 0; matrix products, arithmetic and copies ran while one was open for 0% -> 0% of each run, Pallas kernels for 0% -> 0%
where the time goes in v4:
time: 50.4 us; the launch traced here: 50.2 us
  Pallas kernels  48.8 us (97%)
  local copies, waits for them, and re-layouts  0.73 us (1%)
  between operations  0.65 us (1%)
    pallas_call x1, Pallas kernels, finish(): pl.pallas_call(finish_kernel, name='finish', out_shape=pltpu.VMEM((rows,...  35 us
    pallas_call x1, Pallas kernels, attend(): pl.pallas_call(functools.partial(attn_kernel, sp_size), name='attend', ou...  13.8 us

profile of v4, /device:TPU:0, one launch (start us, length us, event | category | flops | bytes accessed | tf_op | source)
XLA Modules:
  0.0 50.2 jit_solution(15290041616975845212)
XLA Ops:
  0.6 13.8 %attend.1 = (bf16[64,256,256]{2,1,0:T(8,128)(2,1)}, bf16[64,256,256]{2,1,0:T(8,128)(2,1)}, f32[4,32,384]{2,1,0:T(8,128)S(1)}) custom-call(s32[64]{0:T(128)} %pos_hbm.1, f32[1,128]{1,0:T(1,128)} %constant.5.freq_hbm, bf16[64,2560]{1,0:T(8,128)(2,1)} %tok_hbm.3, bf16[2560]{0:T(1024)(128)(2,1)} %gain_hbm.2, bf16[2560,512]{1,0:T(8,128)(2,1)} %wq_hbm.1, ...), custom_call_target="tpu_custom_call" | custom-call | flops 335544320 | bytes 23068672 | tf_op jit(solution)/shard_map/attend/pallas_call | solution.py:149
  14.5 35.0 %finish.1 = bf16[64,2560]{1,0:T(8,128)(2,1)S(1)} custom-call(f32[4,32,384]{2,1,0:T(8,128)S(1)} %get-tuple-element.6.part_ref, bf16[64,2560]{1,0:T(8,128)(2,1)} %tok_hbm.3, bf16[2560]{0:T(1024)(128)(2,1)} %gain_hbm.3, bf16[512,2560]{1,0:T(8,128)(2,1)} %wo_hbm.1, bf16[2560,2560]{1,0:T(8,128)(2,1)} %wg_hbm.1, bf16[2560,2560]{1,0:T(8,128)(2,1)} %wu_hbm.1, ...), custom_call_target="tpu_custom_call" | custom-call | flops 629145600 | bytes 44040192 | tf_op jit(solution)/shard_map/finish/pallas_call | solution.py:429
  49.5 0.7 %copy.20 = bf16[64,2560]{1,0:T(8,128)(2,1)} copy(bf16[64,2560]{1,0:T(8,128)(2,1)S(1)} %finish.1) | data formatting | bytes 655360

commit v5 on v4

v5 whole, which is shorter than its diff:
```python
import functools
import math

import jax
import jax.numpy as jnp
import numpy as np
from jax import lax
from jax.experimental import pallas as pl
from jax.experimental.pallas import tpu as pltpu
from jax.sharding import PartitionSpec as P

NORM_EPS = 1e-5
ROPE_THETA = 10000.0
F32 = jnp.float32
BF16 = jnp.bfloat16
CHUNK = 16


def in_hbm(*arrays):
    return [pltpu.with_memory_space_constraint(x, pltpu.HBM) for x in arrays]


def partner(index, k):
    if k == 0:
        return index
    if k == 1:
        return index + 1 - 2 * lax.rem(index, 2)
    if k == 2:
        return lax.rem(index + 2, 4)
    return 3 - index


def layer_kernel(pos_hbm, freq_hbm, tok_hbm, gain_hbm, wq_hbm, wk_hbm, wv_hbm, ck_hbm, cv_hbm,
                 gain2_hbm, wo_hbm, wg_hbm, wu_hbm, wd_hbm, nk_ref, nv_ref, knew, vnew, out_ref,
                 pos_ref, freq_ref, tok, gain, gain2, qs, posm, part, wo, wg, wu, wd, r1, y2, r2, norm, ms, fin, normed,
                 sem_w, sem_l, sem_k, sem_v, s1, g1, s2, g2, s3, g3, s4, g4, s5z, g5z, s5y, g5y, s5c, g5c):
    s = lax.axis_index("sp")
    z = lax.axis_index("tp")
    line, core = s // 2, lax.rem(s, 2)
    width = wo.shape[1]
    own_rows = CHUNK
    rows = tok.shape[0]
    local_slots, dim = nk_ref.shape[1:]
    half = dim // 2
    chunks = rows // CHUNK
    slots = local_slots * chunks
    base = s * local_slots
    kv_width, q_width = wk_hbm.shape[1], wq_hbm.shape[1]
    wk, wv, wq = wd.at[:, 0:kv_width], wd.at[:, kv_width:2 * kv_width], wd.at[:, 2 * kv_width:2 * kv_width + q_width]
    owner = (core == 1) & ((z == 1) | (z == 2))
    tile = jnp.clip(z - 1, 0, 1)

    loads = [pltpu.make_async_copy(src, dst, sem_w.at[i]) for i, (src, dst) in enumerate((
        (tok_hbm, tok), (gain_hbm, gain), (wk_hbm, wk), (wv_hbm, wv), (wq_hbm, wq), (pos_hbm, pos_ref), (freq_hbm, freq_ref),
        (gain2_hbm, gain2)))]
    for i in (5, 6, 0, 1, 2, 3, 4, 7):
        loads[i].start()
    late = [pltpu.make_async_copy(src, dst, sem_l.at[i]) for i, (src, dst) in enumerate((
        (wo_hbm, wo), (wg_hbm, wg), (wu_hbm, wu), (wd_hbm, wd)))]
    order = [partner(s, k) for k in (3, 2, 1, 0)]
    k_loads, v_loads = [], []
    for c, d in enumerate(order):
        span = pl.ds(pl.multiple_of(d * CHUNK, CHUNK), CHUNK)
        k_loads.append(pltpu.make_async_copy(ck_hbm.at[span], nk_ref.at[span], sem_k.at[c]))
        v_loads.append(pltpu.make_async_copy(cv_hbm.at[span], nv_ref.at[span], sem_v.at[c]))

    def is_owner(t):
        return (core == 1) & (z == t + 1)

    barrier = pltpu.get_barrier_semaphore()
    for k in (1, 2, 3):
        pl.semaphore_signal(barrier, inc=1, device_id={"sp": partner(s, k), "tp": z}, device_id_type=MESH)
    for t in range(2):
        @pl.when(z != t + 1)
        def _():
            pl.semaphore_signal(barrier, inc=1, device_id={"sp": 2 * line + 1, "tp": t + 1}, device_id_type=MESH)

    @pl.when(owner)
    def _():
        for k in (1, 2, 3):
            pl.semaphore_signal(barrier, inc=1, device_id={"sp": 2 * line, "tp": partner(z, k)}, device_id_type=MESH)
        for k in (1, 2):
            pl.semaphore_signal(barrier, inc=1, device_id={"sp": 2 * line + 1, "tp": partner(z, k)}, device_id_type=MESH)

    def remote(src, dst, send_sem, recv_sem, sp, tp):
        return pltpu.make_async_remote_copy(src_ref=src, dst_ref=dst, send_sem=send_sem, recv_sem=recv_sem,
                                            device_id={"sp": sp, "tp": tp}, device_id_type=MESH)

    loads[5].wait()
    loads[6].wait()
    sub = lax.broadcasted_iota(jnp.int32, (8, 128), 0)
    for g in range(rows // 8):
        acc = jnp.zeros((8, 128), jnp.int32)
        for r in range(8):
            acc = jnp.where(sub == r, pos_ref[8 * g + r], acc)
        posm[pl.ds(8 * g, 8), :] = acc
    angles = posm[...].astype(F32) * freq_ref[...]
    cos = jnp.cos(angles)
    sin = jnp.sin(angles)

    loads[0].wait()
    loads[1].wait()
    for r in range(rows // 16):
        wide = tok[16 * r:16 * r + 16, :].astype(F32)
        inv_rms = lax.rsqrt(jnp.mean(wide * wide, axis=-1, keepdims=True) + NORM_EPS)
        normed[16 * r:16 * r + 16, :] = (wide * inv_rms * gain[...].astype(F32).reshape(1, -1)).astype(BF16)

    def fetch(c):
        if c < chunks:
            k_loads[c].start()
            v_loads[c].start()

    def rope(lin):
        a, b = lin[:, :half], lin[:, half:]
        return jnp.concatenate([a * cos - b * sin, b * cos + a * sin], axis=-1)

    loads[2].wait()
    fetch(0)
    knew[...] = rope(jnp.dot(normed[...], wk[...], preferred_element_type=F32)).astype(BF16).astype(F32)
    loads[3].wait()
    vnew[...] = jnp.dot(normed[...], wv[...], preferred_element_type=F32).astype(BF16).astype(F32)
    loads[4].wait()
    fetch(1)
    heads = q_width // dim
    q_lin = jnp.dot(normed[...], wq[...], preferred_element_type=F32)
    q_rot = [rope(q_lin[:, h * dim:(h + 1) * dim]) for h in range(heads)]
    for g in range(rows // 8):
        qs[g] = jnp.concatenate([q_rot[h][8 * g:8 * g + 8] for h in range(heads)], axis=0).astype(BF16)

    sub16 = lax.broadcasted_iota(jnp.int32, (16, dim), 0)
    lane = lax.broadcasted_iota(jnp.int32, (16, local_slots), 1) + base
    lane128 = lax.broadcasted_iota(jnp.int32, (16, 128), 1)

    def spread_lanes(x):
        return jnp.concatenate([x] * (local_slots // 128), axis=1)

    def twice(x):
        return jnp.concatenate([x, x], axis=0)

    first = []
    for c, d in enumerate(order):
        k_loads[c].wait()
        fetch(c + 2)
        if c == chunks - 1:
            late[0].start()
            late[1].start()
        probs = []
        for u in range(CHUNK // 8):
            query = qs[2 * d + u]
            scores = jnp.zeros((16, local_slots), F32)
            for j in range(8):
                one = lax.dot_general(query, nk_ref[CHUNK * d + 8 * u + j], (((1,), (1,)), ((), ())), preferred_element_type=F32)
                scores = jnp.where(jnp.bitwise_and(sub16, 7) == j, one, scores)
            eight = pl.ds(pl.multiple_of(CHUNK * d + 8 * u, 8), 8)
            pos16 = twice(posm[eight, :])
            hit = lane == spread_lanes(jnp.bitwise_and(pos16, slots - 1))
            fresh = jnp.sum(query.astype(F32) * twice(knew[eight, :]), axis=-1, keepdims=True)
            scores = jnp.where(hit, fresh, scores) * (1.0 / math.sqrt(dim))
            valid = lane <= spread_lanes(jnp.where(pos16 >= slots - 1, slots, pos16))
            top = jnp.max(jnp.where(valid, scores, -jnp.inf), axis=-1, keepdims=True)
            safe = jnp.where(top == -jnp.inf, 0.0, top)
            weights = jnp.exp(jnp.where(valid, scores - safe, -jnp.inf))
            share = jnp.sum(weights, axis=-1, keepdims=True)
            chosen = jnp.sum(jnp.where(hit, weights, 0.0), axis=-1, keepdims=True).astype(BF16).astype(F32)
            probs.append((u, eight, jnp.where(hit, 0.0, weights).astype(BF16), chosen, top, share))
        v_loads[c].wait()
        if c == chunks - 1:
            late[2].start()
            late[3].start()
        for u, eight, weights, chosen, top, share in probs:
            out = jnp.zeros((16, dim), F32)
            for j in range(8):
                one = jnp.dot(weights, nv_ref[CHUNK * d + 8 * u + j], preferred_element_type=F32)
                out = jnp.where(jnp.bitwise_and(sub16, 7) == j, one, out)
            out = out + chosen * twice(vnew[eight, :])
            stats = jnp.where(lane128 < 64, top, share)
            for h in range(heads):
                part[chunks - 1 - c, 16 * h + 8 * u:16 * h + 8 * u + 8, 0:dim] = out[8 * h:8 * h + 8]
                part[chunks - 1 - c, 16 * h + 8 * u:16 * h + 8 * u + 8, dim:dim + 128] = stats[8 * h:8 * h + 8]
        if c == 0:
            middle = (z == 1) | (z == 2)
            pl.semaphore_wait(barrier, jnp.where(middle, jnp.where(core == 1, 9, 4), 5))
        k = chunks - 1 - c
        if k:
            first.append(remote(part.at[k], r1.at[k - 1], s1.at[k - 1], g1.at[k - 1], partner(s, k), z))
            first[-1].start()
    loads[7].wait()

    def to_owner(t, c, cut, rows, sums, send_sem, recv_sem):
        span = pl.ds(*cut[c])
        return remote(rows.at[t, :, span], sums.at[core, z, :, span], send_sem.at[t, c], recv_sem.at[core, z, c], 2 * line + 1, t + 1)

    def send_sums(value, c, cut, rows, sums, send_sem, recv_sem):
        at, size = cut[c]
        for t in range(2):
            rows[t, :, at:at + size] = value[8 * t:8 * t + 8]
        for t in range(2):
            @pl.when(jnp.logical_not(is_owner(t)))
            def _():
                to_owner(t, c, cut, rows, sums, send_sem, recv_sem).start()

    def wait_sums(c, cut, rows, sums, send_sem, recv_sem):
        at, size = cut[c]
        span = pl.ds(at, size)
        sums[1, z, :, at:at + size] = rows[tile, :, at:at + size]
        for b in range(2):
            for k in (1, 3, 2, 0):
                if b == 0 or k:
                    far = partner(z, k)
                    remote(rows.at[0, :, span], sums.at[b, far, :, span], send_sem.at[0, c], recv_sem.at[b, far, c], 2 * line + b, far).wait_recv()
        return [sums[b, 0, :, at:at + size] + sums[b, 1, :, at:at + size] + sums[b, 2, :, at:at + size] + sums[b, 3, :, at:at + size]
                for b in range(2)]

    def sent_sums(cut, rows, sums, send_sem, recv_sem):
        for t in range(2):
            @pl.when(jnp.logical_not(is_owner(t)))
            def _():
                for c in range(len(cut)):
                    to_owner(t, c, cut, rows, sums, send_sem, recv_sem).wait_send()

    for copy in first:
        copy.wait_recv()
    parts = [part[0], r1[0], r1[1], r1[2]]
    tops = [p[:, dim:dim + 1] for p in parts]
    shares = [p[:, dim + 64:dim + 65] for p in parts]
    top = jnp.maximum(jnp.maximum(tops[0], tops[1]), jnp.maximum(tops[2], tops[3]))
    scales = [jnp.exp(t - top) for t in tops]
    total = sum(f * l for f, l in zip(scales, shares))
    mixed = sum(f * p[:, :dim] for f, p in zip(scales, parts)) / total
    att = jnp.concatenate([mixed[:own_rows], mixed[own_rows:]], axis=1).astype(BF16)

    late[0].wait()
    for c, (at, size) in enumerate(CUT_O):
        send_sums(jnp.dot(att, wo[:, at:at + size], preferred_element_type=F32), c, CUT_O, y2, r2, s2, g2)

    def spread(b, k, c):
        span = pl.ds(*CUT_M[c])
        return remote(ms.at[tile, :, span] if b else norm.at[:, span], ms.at[tile, :, span], s3.at[b, k, c], g3.at[tile, c], 2 * line + b, partner(z, k))

    @pl.when(owner)
    def _():
        halves = [wait_sums(c, CUT_O, y2, r2, s2, g2) for c in range(len(CUT_O))]
        for b in range(2):
            mine = tok[pl.ds(pl.multiple_of((2 * line + b) * own_rows, own_rows), own_rows), :].astype(F32)
            mine = jnp.where(tile == 0, mine[0:8], mine[8:16])
            hidden = (mine + jnp.concatenate([h[b] for h in halves], axis=1)).astype(BF16).astype(F32)
            inv_rms = lax.rsqrt(jnp.mean(hidden * hidden, axis=-1, keepdims=True) + NORM_EPS)
            scaled = (hidden * inv_rms * gain2[...].astype(F32).reshape(1, -1)).astype(BF16).astype(F32)
            fin[line, tile, b] = hidden
            if b == 0:
                norm[...] = scaled
            else:
                ms[tile] = scaled
        for c in range(len(CUT_M)):
            for k in (2, 3, 1, 0):
                for b in (0, 1):
                    if b == 0 or k:
                        spread(b, k, c).start()

    late[1].wait()
    late[2].wait()
    gate = up = None
    for c, (at, size) in enumerate(CUT_M):
        span = pl.ds(at, size)
        for t in range(2):
            @pl.when(jnp.logical_not(is_owner(t)))
            def _():
                remote(norm.at[:, span], ms.at[t, :, span], s3.at[0, 0, c], g3.at[t, c], 2 * line + 1, t + 1).wait_recv()
        rows = jnp.concatenate([ms[0, :, at:at + size], ms[1, :, at:at + size]], axis=0).astype(BF16)
        pair = [jnp.dot(rows, w[at:at + size, :], preferred_element_type=F32) for w in (wg, wu)]
        gate = pair[0] if gate is None else gate + pair[0]
        up = pair[1] if up is None else up + pair[1]
    act = gate * (1.0 / (1.0 + jnp.exp(-gate))) * up
    act = act.astype(BF16)

    late[3].wait()
    sent_sums(CUT_O, y2, r2, s2, g2)
    for c, (at, size) in enumerate(CUT_D):
        send_sums(jnp.dot(act, wd[:, at:at + size], preferred_element_type=F32), c, CUT_D, y2, r2, s4, g4)

    def along(t, k, c):
        span = pl.ds(*CUT_D[c])
        rows = fin.at[line, t, :, :, span]
        return remote(rows, rows, s5z.at[k, c], g5z.at[t, c], s, partner(z, k))

    def across(t, c):
        span = pl.ds(*CUT_D[c])
        rows = fin.at[line, t, :, :, span]
        return remote(rows, rows, s5y.at[t, c], g5y.at[t, c], partner(s, 2), z)

    def beside(far, t, c):
        span = pl.ds(*CUT_D[c])
        rows = fin.at[line if far == 0 else 1 - line, t, :, :, span]
        return remote(rows, rows, s5c.at[far, t, c], g5c.at[far, t, c], partner(s, 1), z)

    @pl.when(owner)
    def _():
        for c, (at, size) in enumerate(CUT_D):
            totals = wait_sums(c, CUT_D, y2, r2, s4, g4)
            for b in range(2):
                fin[line, tile, b, :, at:at + size] = (fin[line, tile, b, :, at:at + size] + totals[b]).astype(BF16).astype(F32)
            for k in (2, 3, 1):
                along(tile, k, c).start()
            across(tile, c).start()
            beside(0, tile, c).start()

    @pl.when(core == 1)
    def _():
        for c in range(len(CUT_D)):
            for t in range(2):
                @pl.when(z != t + 1)
                def _():
                    along(t, 1, c).wait_recv()
                    across(t, c).start()
                    beside(0, t, c).start()
        for c in range(len(CUT_D)):
            for t in range(2):
                span = pl.ds(*CUT_D[c])
                rows = fin.at[1 - line, t, :, :, span]
                remote(rows, rows, s5y.at[t, c], g5y.at[t, c], partner(s, 2), z).wait_recv()
                beside(1, t, c).start()

    @pl.when(core == 0)
    def _():
        for far in range(2):
            for c in range(len(CUT_D)):
                for t in range(2):
                    beside(far, t, c).wait_recv()

    for y in range(2):
        for b in range(2):
            out_ref[pl.ds(own_rows * (2 * y + b), own_rows), :] = jnp.concatenate([fin[y, 0, b], fin[y, 1, b]], axis=0).astype(BF16)

    for copy in first:
        copy.wait_send()
    sent_sums(CUT_D, y2, r2, s4, g4)

    @pl.when(owner)
    def _():
        for c in range(len(CUT_M)):
            for k in range(4):
                for b in range(2):
                    if b == 0 or k:
                        spread(b, k, c).wait_send()
        for c in range(len(CUT_D)):
            for k in (1, 2, 3):
                along(tile, k, c).wait_send()

    @pl.when(core == 1)
    def _():
        for c in range(len(CUT_D)):
            for t in range(2):
                across(t, c).wait_send()
                beside(0, t, c).wait_send()
                beside(1, t, c).wait_send()


MESH = pl.DeviceIdType.MESH
CUT_O = ((0, 512), (512, 2048))
CUT_M = ((0, 512), (512, 512), (1024, 512), (1536, 512), (2048, 512))
CUT_D = ((0, 512), (512, 512), (1024, 512), (1536, 512), (2048, 512))


def layer(tokens, positions, cache_k, cache_v, gain, w_q, w_k, w_v, w_o, gain2, w_gate, w_up, w_down):
    rows, width = tokens.shape
    _, local_slots, _, dim = cache_k.shape
    heads = w_q.shape[1] // dim
    freq = (ROPE_THETA ** (-2.0 * np.arange(dim // 2, dtype=np.float64) / dim)).astype(np.float32)
    ck = cache_k.reshape(rows, local_slots, dim)
    cv = cache_v.reshape(rows, local_slots, dim)
    hbm = pl.BlockSpec(memory_space=pltpu.HBM)
    vmem = pl.BlockSpec(memory_space=pltpu.VMEM)
    dma = pltpu.SemaphoreType.DMA
    chunks = rows // CHUNK
    share = (heads * CHUNK, dim + 128)
    cut_o, cut_m, cut_d = len(CUT_O), len(CUT_M), len(CUT_D)
    return pl.pallas_call(
        layer_kernel,
        name="layer",
        out_shape=(pltpu.VMEM(ck.shape, BF16), pltpu.VMEM(cv.shape, BF16), pltpu.VMEM((rows, dim), F32),
                   pltpu.VMEM((rows, dim), F32), pltpu.VMEM((rows, width), BF16)),
        in_specs=[hbm] * 14,
        out_specs=[vmem] * 5,
        scratch_shapes=[
            pltpu.SMEM((rows,), jnp.int32),
            pltpu.VMEM((1, dim // 2), F32),
            pltpu.VMEM((rows, width), BF16),
            pltpu.VMEM((width,), BF16),
            pltpu.VMEM((width,), BF16),
            pltpu.VMEM((rows // 8, 8 * heads, dim), BF16),
            pltpu.VMEM((rows, 128), jnp.int32),
            pltpu.VMEM((chunks,) + share, F32),
            pltpu.VMEM(w_o.shape, BF16),
            pltpu.VMEM(w_gate.shape, BF16),
            pltpu.VMEM(w_up.shape, BF16),
            pltpu.VMEM(w_down.shape, BF16),
            pltpu.VMEM((3,) + share, F32),
            pltpu.VMEM((2, 8, width), F32),
            pltpu.VMEM((2, 4, 8, width), F32),
            pltpu.VMEM((8, width), F32),
            pltpu.VMEM((2, 8, width), F32),
            pltpu.VMEM((2, 2, 2, 8, width), F32),
            pltpu.VMEM((rows, width), BF16),
            dma((8,)), dma((4,)), dma((chunks,)), dma((chunks,)),
            dma((3,)), dma((3,)),
            dma((2, cut_o)), dma((2, 4, cut_o)),
            dma((2, 4, cut_m)), dma((2, cut_m)),
            dma((2, cut_d)), dma((2, 4, cut_d)),
            dma((4, cut_d)), dma((2, cut_d)),
            dma((2, cut_d)), dma((2, cut_d)),
            dma((2, 2, cut_d)), dma((2, 2, cut_d)),
        ],
        compiler_params=pltpu.CompilerParams(collective_id=0, has_side_effects=True, vmem_limit_bytes=VMEM_LAYER),
        cost_estimate=pl.CostEstimate(flops=2 * 16 * width * 2560 * 3, bytes_accessed=64 << 20, transcendentals=0),
    )(*in_hbm(positions, jnp.asarray(freq).reshape(1, -1), tokens, gain, w_q, w_k, w_v, ck, cv, gain2, w_o, w_gate, w_up, w_down))


def store_kernel(slots, pos_hbm, row_ref, knew, vnew, k_in, v_in, nk_ref, nv_ref, out_hbm, nk_hbm, nv_hbm, pos_ref, sem_p, sem_o, sem_k, sem_v):
    rows, local_slots, dim = nk_ref.shape
    base = lax.axis_index("sp") * local_slots
    fetch = pltpu.make_async_copy(pos_hbm, pos_ref, sem_p)
    fetch.start()
    out_copy = pltpu.make_async_copy(row_ref, out_hbm, sem_o)
    out_copy.start()
    sub16 = lax.broadcasted_iota(jnp.int32, (16, dim), 0)
    fetch.wait()

    def patch(ref, new_ref, b):
        offset = jnp.bitwise_and(pos_ref[b], slots - 1) - base
        inside = jnp.clip(offset, 0, local_slots - 1)
        start = pl.multiple_of((inside // 16) * 16, 16)
        old = ref[b, pl.ds(start, 16), :].astype(F32)
        ref[b, pl.ds(start, 16), :] = jnp.where(sub16 == offset - start, new_ref[pl.ds(b, 1), :], old).astype(BF16)

    stores = []
    for c in range(rows // CHUNK):
        span = pl.ds(c * CHUNK, CHUNK)
        for ref, new_ref, dst, sem in ((nk_ref, knew, nk_hbm, sem_k), (nv_ref, vnew, nv_hbm, sem_v)):
            for j in range(CHUNK):
                patch(ref, new_ref, c * CHUNK + j)
            stores.append(pltpu.make_async_copy(ref.at[span], dst.at[span], sem.at[c]))
            stores[-1].start()
    for copy in stores:
        copy.wait()
    out_copy.wait()


def store(positions, row, knew, vnew, nk, nv, slots):
    hbm = pl.BlockSpec(memory_space=pltpu.HBM)
    vmem = pl.BlockSpec(memory_space=pltpu.VMEM)
    dma = pltpu.SemaphoreType.DMA
    chunks = nk.shape[0] // CHUNK
    return pl.pallas_call(
        functools.partial(store_kernel, slots),
        name="store",
        out_shape=(pltpu.VMEM(nk.shape, BF16), pltpu.VMEM(nv.shape, BF16), jax.ShapeDtypeStruct(row.shape, BF16),
                   jax.ShapeDtypeStruct(nk.shape, BF16), jax.ShapeDtypeStruct(nv.shape, BF16)),
        in_specs=[hbm] + [vmem] * 5,
        out_specs=[vmem, vmem, hbm, hbm, hbm],
        input_output_aliases={4: 0, 5: 1},
        scratch_shapes=[pltpu.SMEM(positions.shape, jnp.int32), dma, dma, dma((chunks,)), dma((chunks,))],
        compiler_params=pltpu.CompilerParams(vmem_limit_bytes=VMEM_STORE),
    )(*in_hbm(positions), row, knew, vnew, nk, nv)[2:]


VMEM_LAYER = 48620 << 10
VMEM_STORE = 4 << 20


def solution(mesh):
    sp_size = mesh.shape["sp"]
    cache_spec = P("dp", "sp", "tp", None)
    row_spec = P("dp", None)
    col_spec = P(None, "tp")
    in_specs = (row_spec, P("dp"), cache_spec, cache_spec, P(None), col_spec, col_spec, col_spec, P("tp", None), P(None), col_spec, col_spec, P("tp", None))
    out_specs = (row_spec, cache_spec, cache_spec)

    def local_step(tokens, positions, cache_k, cache_v, attn_gain, w_q, w_k, w_v, w_o, mlp_gain, w_gate, w_up, w_down):
        nk, nv, knew, vnew, row = layer(tokens, positions, cache_k, cache_v, attn_gain, w_q, w_k, w_v, w_o, mlp_gain, w_gate, w_up, w_down)
        layer_out, new_k, new_v = store(positions, row, knew, vnew, nk, nv, sp_size * cache_k.shape[1])
        return layer_out, new_k.reshape(cache_k.shape), new_v.reshape(cache_v.shape)

    return jax.shard_map(local_step, mesh=mesh, in_specs=in_specs, out_specs=out_specs, check_vma=False)
```

time: 50.4 us -> 47.3 us (0.938)
  Pallas kernels: 48.8 us -> 46.5 us
  local copies, waits for them, and re-layouts: 0.73 us -> 0 us
    pallas_call x2, Pallas kernels: 48.8 us -> 46.5 us  [the longest x1 39.7 us: layer(): pl.pallas_call(layer_kernel, name='layer', out_shape=(pltpu.VMEM(ck.shape...]
    unnamed x1 -> x0, local copies, waits for them, and re-layouts: 0.73 us -> none
where the time goes in v5:
time: 47.3 us; the launch traced here: 47.1 us
  Pallas kernels  46.5 us (98%)
  between operations  0.64 us (1%)
    pallas_call x1, Pallas kernels, layer(): pl.pallas_call(layer_kernel, name='layer', out_shape=(pltpu.VMEM(ck.shape...  39.7 us
    pallas_call x1, Pallas kernels, store(): pl.pallas_call(functools.partial(store_kernel, slots), name='store', out_...  6.72 us

profile of v5, /device:TPU:0, one launch (start us, length us, event | category | flops | bytes accessed | tf_op | source)
XLA Modules:
  0.0 47.1 jit_solution(13816595542123481245)
XLA Ops:
  0.6 39.7 %layer.1 = (bf16[64,256,256]{2,1,0:T(8,128)(2,1)S(1)}, bf16[64,256,256]{2,1,0:T(8,128)(2,1)S(1)}, f32[64,256]{1,0:T(8,128)S(1)}, f32[64,256]{1,0:T(8,128)S(1)}, bf16[64,2560]{1,0:T(8,128)(2,1)S(1)}) custom-call(s32[64]{0:T(128)} %pos_hbm.3, f32[1,128]{1,0:T(1,128)} %constant.5.freq_hbm, bf16[64,2560]{1,0:T(8,128)(2,1)} %tok_hbm.1, bf16[2560]{0:T(1024)(128)(2,1)} %gain_hbm.1, ...), custom_call_target="tpu_custom_call" | custom-call | flops 629145600 | bytes 67108864 | tf_op jit(solution)/shard_map/layer/pallas_call | solution.py:377
  40.4 6.7 %store.1 = (bf16[64,256,256]{2,1,0:T(8,128)(2,1)S(1)}, bf16[64,256,256]{2,1,0:T(8,128)(2,1)S(1)}, bf16[64,2560]{1,0:T(8,128)(2,1)}, bf16[64,256,256]{2,1,0:T(8,128)(2,1)}, bf16[64,256,256]{2,1,0:T(8,128)(2,1)}) custom-call(s32[64]{0:T(128)} %pos_hbm.3, bf16[64,2560]{1,0:T(8,128)(2,1)S(1)} %get-tuple-element.11.row_ref, ...), custom_call_target="tpu_custom_call", output_to_operand_aliasing={{0}: (4, {}), {1}: (5, {})} | custom-call | tf_op jit(solution)/shard_map/store/pallas_call | solution.py:453

commit v6 on v5

--- a/solution.py
+++ b/solution.py
@@ -31,8 +31,8 @@
 
 
 def layer_kernel(pos_hbm, freq_hbm, tok_hbm, gain_hbm, wq_hbm, wk_hbm, wv_hbm, ck_hbm, cv_hbm,
-                 gain2_hbm, wo_hbm, wg_hbm, wu_hbm, wd_hbm, nk_ref, nv_ref, knew, vnew, out_ref,
-                 pos_ref, freq_ref, tok, gain, gain2, qs, posm, part, wo, wg, wu, wd, r1, y2, r2, norm, ms, fin, normed,
+                 gain2_hbm, wo_hbm, wg_hbm, wu_hbm, wd_hbm, nk_ref, nv_ref, knew, vnew, out_ref, pos_ref,
+                 freq_ref, tok, gain, gain2, qs, posm, part, wo, wg, wu, wd, r1, y2, r2, norm, ms, fin, normed,
                  sem_w, sem_l, sem_k, sem_v, s1, g1, s2, g2, s3, g3, s4, g4, s5z, g5z, s5y, g5y, s5c, g5c):
     s = lax.axis_index("sp")
     z = lax.axis_index("tp")
@@ -57,7 +57,8 @@
         loads[i].start()
     late = [pltpu.make_async_copy(src, dst, sem_l.at[i]) for i, (src, dst) in enumerate((
         (wo_hbm, wo), (wg_hbm, wg), (wu_hbm, wu), (wd_hbm, wd)))]
-    order = [partner(s, k) for k in (3, 2, 1, 0)]
+    turns = (2, 3, 1, 0)
+    order = [partner(s, k) for k in turns]
     k_loads, v_loads = [], []
     for c, d in enumerate(order):
         span = pl.ds(pl.multiple_of(d * CHUNK, CHUNK), CHUNK)
@@ -166,7 +167,6 @@
         v_loads[c].wait()
         if c == chunks - 1:
             late[2].start()
-            late[3].start()
         for u, eight, weights, chosen, top, share in probs:
             out = jnp.zeros((16, dim), F32)
             for j in range(8):
@@ -175,12 +175,12 @@
             out = out + chosen * twice(vnew[eight, :])
             stats = jnp.where(lane128 < 64, top, share)
             for h in range(heads):
-                part[chunks - 1 - c, 16 * h + 8 * u:16 * h + 8 * u + 8, 0:dim] = out[8 * h:8 * h + 8]
-                part[chunks - 1 - c, 16 * h + 8 * u:16 * h + 8 * u + 8, dim:dim + 128] = stats[8 * h:8 * h + 8]
+                part[turns[c], 16 * h + 8 * u:16 * h + 8 * u + 8, 0:dim] = out[8 * h:8 * h + 8]
+                part[turns[c], 16 * h + 8 * u:16 * h + 8 * u + 8, dim:dim + 128] = stats[8 * h:8 * h + 8]
         if c == 0:
             middle = (z == 1) | (z == 2)
             pl.semaphore_wait(barrier, jnp.where(middle, jnp.where(core == 1, 9, 4), 5))
-        k = chunks - 1 - c
+        k = turns[c]
         if k:
             first.append(remote(part.at[k], r1.at[k - 1], s1.at[k - 1], g1.at[k - 1], partner(s, k), z))
             first[-1].start()
@@ -194,7 +194,8 @@
         at, size = cut[c]
         for t in range(2):
             rows[t, :, at:at + size] = value[8 * t:8 * t + 8]
-        for t in range(2):
+        crossing = jnp.where(z < 2, 1, 0)
+        for t in (crossing, 1 - crossing):
             @pl.when(jnp.logical_not(is_owner(t)))
             def _():
                 to_owner(t, c, cut, rows, sums, send_sem, recv_sem).start()
@@ -259,6 +260,7 @@
 
     late[1].wait()
     late[2].wait()
+    late[3].start()
     gate = up = None
     for c, (at, size) in enumerate(CUT_M):
         span = pl.ds(at, size)
@@ -357,7 +359,7 @@
 
 MESH = pl.DeviceIdType.MESH
 CUT_O = ((0, 512), (512, 2048))
-CUT_M = ((0, 512), (512, 512), (1024, 512), (1536, 512), (2048, 512))
+CUT_M = ((0, 256), (256, 512), (768, 768), (1536, 1024))
 CUT_D = ((0, 512), (512, 512), (1024, 512), (1536, 512), (2048, 512))
 
 
@@ -378,11 +380,10 @@
         layer_kernel,
         name="layer",
         out_shape=(pltpu.VMEM(ck.shape, BF16), pltpu.VMEM(cv.shape, BF16), pltpu.VMEM((rows, dim), F32),
-                   pltpu.VMEM((rows, dim), F32), pltpu.VMEM((rows, width), BF16)),
+                   pltpu.VMEM((rows, dim), F32), pltpu.VMEM((rows, width), BF16), pltpu.SMEM((rows,), jnp.int32)),
         in_specs=[hbm] * 14,
-        out_specs=[vmem] * 5,
+        out_specs=[vmem] * 5 + [pl.BlockSpec(memory_space=pltpu.SMEM)],
         scratch_shapes=[
-            pltpu.SMEM((rows,), jnp.int32),
             pltpu.VMEM((1, dim // 2), F32),
             pltpu.VMEM((rows, width), BF16),
             pltpu.VMEM((width,), BF16),
@@ -415,15 +416,12 @@
     )(*in_hbm(positions, jnp.asarray(freq).reshape(1, -1), tokens, gain, w_q, w_k, w_v, ck, cv, gain2, w_o, w_gate, w_up, w_down))
 
 
-def store_kernel(slots, pos_hbm, row_ref, knew, vnew, k_in, v_in, nk_ref, nv_ref, out_hbm, nk_hbm, nv_hbm, pos_ref, sem_p, sem_o, sem_k, sem_v):
+def store_kernel(slots, pos_ref, row_ref, knew, vnew, k_in, v_in, nk_ref, nv_ref, out_hbm, nk_hbm, nv_hbm, sem_o, sem_k, sem_v):
     rows, local_slots, dim = nk_ref.shape
     base = lax.axis_index("sp") * local_slots
-    fetch = pltpu.make_async_copy(pos_hbm, pos_ref, sem_p)
-    fetch.start()
     out_copy = pltpu.make_async_copy(row_ref, out_hbm, sem_o)
     out_copy.start()
     sub16 = lax.broadcasted_iota(jnp.int32, (16, dim), 0)
-    fetch.wait()
 
     def patch(ref, new_ref, b):
         offset = jnp.bitwise_and(pos_ref[b], slots - 1) - base
@@ -445,7 +443,7 @@
     out_copy.wait()
 
 
-def store(positions, row, knew, vnew, nk, nv, slots):
+def store(places, row, knew, vnew, nk, nv, slots):
     hbm = pl.BlockSpec(memory_space=pltpu.HBM)
     vmem = pl.BlockSpec(memory_space=pltpu.VMEM)
     dma = pltpu.SemaphoreType.DMA
@@ -455,12 +453,12 @@
         name="store",
         out_shape=(pltpu.VMEM(nk.shape, BF16), pltpu.VMEM(nv.shape, BF16), jax.ShapeDtypeStruct(row.shape, BF16),
                    jax.ShapeDtypeStruct(nk.shape, BF16), jax.ShapeDtypeStruct(nv.shape, BF16)),
-        in_specs=[hbm] + [vmem] * 5,
+        in_specs=[pl.BlockSpec(memory_space=pltpu.SMEM)] + [vmem] * 5,
         out_specs=[vmem, vmem, hbm, hbm, hbm],
         input_output_aliases={4: 0, 5: 1},
-        scratch_shapes=[pltpu.SMEM(positions.shape, jnp.int32), dma, dma, dma((chunks,)), dma((chunks,))],
+        scratch_shapes=[dma, dma((chunks,)), dma((chunks,))],
         compiler_params=pltpu.CompilerParams(vmem_limit_bytes=VMEM_STORE),
-    )(*in_hbm(positions), row, knew, vnew, nk, nv)[2:]
+    )(places, row, knew, vnew, nk, nv)[2:]
 
 
 VMEM_LAYER = 48620 << 10
@@ -476,8 +474,8 @@
     out_specs = (row_spec, cache_spec, cache_spec)
 
     def local_step(tokens, positions, cache_k, cache_v, attn_gain, w_q, w_k, w_v, w_o, mlp_gain, w_gate, w_up, w_down):
-        nk, nv, knew, vnew, row = layer(tokens, positions, cache_k, cache_v, attn_gain, w_q, w_k, w_v, w_o, mlp_gain, w_gate, w_up, w_down)
-        layer_out, new_k, new_v = store(positions, row, knew, vnew, nk, nv, sp_size * cache_k.shape[1])
+        nk, nv, knew, vnew, row, places = layer(tokens, positions, cache_k, cache_v, attn_gain, w_q, w_k, w_v, w_o, mlp_gain, w_gate, w_up, w_down)
+        layer_out, new_k, new_v = store(places, row, knew, vnew, nk, nv, sp_size * cache_k.shape[1])
         return layer_out, new_k.reshape(cache_k.shape), new_v.reshape(cache_v.shape)
 
     return jax.shard_map(local_step, mesh=mesh, in_specs=in_specs, out_specs=out_specs, check_vma=False)

time: 47.3 us -> 46.5 us (0.983)
  Pallas kernels: 46.5 us -> 45.7 us
    pallas_call x1, Pallas kernels: 6.72 us -> 6.15 us  [store(): pl.pallas_call(functools.partial(store_kernel, slots), name='store', out_...]
where the time goes in v6:
time: 46.5 us; the launch traced here: 46.4 us
  Pallas kernels  45.7 us (98%)
  between operations  0.64 us (1%)
    pallas_call x1, Pallas kernels, layer(): pl.pallas_call(layer_kernel, name='layer', out_shape=(pltpu.VMEM(ck.shape...  39.6 us
    pallas_call x1, Pallas kernels, store(): pl.pallas_call(functools.partial(store_kernel, slots), name='store', out_...  6.15 us

profile of v6, /device:TPU:0, one launch (start us, length us, event | category | flops | bytes accessed | tf_op | source)
XLA Modules:
  0.0 46.4 jit_solution(10167173554653798533)
XLA Ops:
  0.6 39.6 %layer.1 = (bf16[64,256,256]{2,1,0:T(8,128)(2,1)S(1)}, bf16[64,256,256]{2,1,0:T(8,128)(2,1)S(1)}, f32[64,256]{1,0:T(8,128)S(1)}, f32[64,256]{1,0:T(8,128)S(1)}, ...) custom-call(s32[64]{0:T(128)} %pos_hbm.1, f32[1,128]{1,0:T(1,128)} %constant.5.freq_hbm, bf16[64,2560]{1,0:T(8,128)(2,1)} %tok_hbm.1, ...), custom_call_target="tpu_custom_call" | custom-call | flops 629145600 | bytes 67108864 | tf_op jit(solution)/shard_map/layer/pallas_call | solution.py:379
  40.2 6.2 %store.1 = (bf16[64,256,256]{2,1,0:T(8,128)(2,1)S(1)}, bf16[64,256,256]{2,1,0:T(8,128)(2,1)S(1)}, bf16[64,2560]{1,0:T(8,128)(2,1)}, bf16[64,256,256]{2,1,0:T(8,128)(2,1)}, bf16[64,256,256]{2,1,0:T(8,128)(2,1)}) custom-call(s32[64]{0:T(128)S(4)} %get-tuple-element.12.pos_ref, ...), custom_call_target="tpu_custom_call", output_to_operand_aliasing={{0}: (4, {}), {1}: (5, {})} | custom-call | tf_op jit(solution)/shard_map/store/pallas_call | solution.py:451
